TPU v7x, 128 devices: a whole 4x4x4 slice. The times are simulated.
128 devices in a mesh: gx: 4 (over x), gy: 4 (over z_lo, core), gz: 8 (over z_hi, y).
Axes of the slice: x: 4, y: 4, z: 4 (z_hi: 2, z_lo: 2; z = z_hi * 2 + z_lo), core: 2. Of those that a mesh axis runs over, the one named last changes fastest.
Arguments:
- orbitals: float32 [16, 48, 48, 1024], P(None, 'gx', 'gy', 'gz'), may hold values from -6 to 6
- potential: float32 [48, 48, 1024], P('gx', 'gy', 'gz'), may hold values from 0 to 2
Outputs:
- filtered: float32 [16, 48, 48, 1024], P(None, 'gx', 'gy', 'gz')
All inputs are finite; a program needn't handle non-finite values.
Results may differ from a plain program's by a relative error of at most 0.00002.
Values sent between devices are 32-bit elements; how exact they have to be, the bound alone decides.
A program may use at most 64 MiB of HBM per device.

v0:
```python
import jax
import jax.numpy as jnp
from jax import lax
from jax.sharding import PartitionSpec as P

DEGREE = 2


SECOND = (
    -5369.0 / 1800.0,
    12.0 / 7.0,
    -15.0 / 56.0,
    10.0 / 189.0,
    -1.0 / 112.0,
    2.0 / 1925.0,
    -1.0 / 16632.0,
)
FIRST = (6.0 / 7.0, -15.0 / 56.0, 5.0 / 63.0, -1.0 / 56.0, 3.0 / 385.0, -1.0 / 792.0)
METRIC = ((1.0, 0.25, 0.15), (0.25, 1.0, 0.2), (0.15, 0.2, 1.0))
CENTER = 10.5
HALF_WIDTH = 9.5


def split_up(value, dim, size):
    lengths = value.shape
    blocks = value.reshape(*lengths[:dim], size, lengths[dim] // size, *lengths[dim + 1 :])
    return jnp.moveaxis(blocks, dim, 0)


def joined_along(blocks, dim):
    lengths = list(blocks.shape[1:])
    lengths[dim] *= blocks.shape[0]
    return jnp.moveaxis(blocks, 0, dim).reshape(lengths)


def one_exchange(value, axis, axes, splits, concats):
    sizes = [lax.axis_size(a) for a in axes]
    blocks = split_up(value, splits[0], sizes[0])
    blocks = jnp.moveaxis(split_up(blocks, splits[1] + 1, sizes[1]), 0, 1)
    inside = blocks.shape[2:]
    blocks = blocks.reshape(-1, *inside)
    blocks = lax.all_to_all(blocks, axis, split_axis=0, concat_axis=0, tiled=True)
    blocks = joined_along(blocks.reshape(*sizes, *inside), concats[0] + 1)
    return joined_along(blocks, concats[1])


def from_everyone(value, axis):
    copies = jnp.broadcast_to(value, (lax.axis_size(axis), *value.shape))
    return lax.all_to_all(copies, axis, split_axis=0, concat_axis=0, tiled=True)


def gather_directly(value, axis, dim):
    blocks = from_everyone(value, axis)
    return joined_along(blocks, dim)


def extended(block, sides, width):
    for axis, dim in sides:
        count = lax.axis_size(axis)
        forward = [(i, i + 1) for i in range(count - 1)]
        forward.append((count - 1, 0))
        backward = [(target, source) for source, target in forward]
        low = lax.ppermute(
            lax.slice_in_dim(block, block.shape[dim] - width, None, axis=dim), axis, forward
        )
        high = lax.ppermute(lax.slice_in_dim(block, 0, width, axis=dim), axis, backward)
        block = jnp.concatenate([low, block, high], axis=dim)
    return block


def window(values, starts, lengths):
    leading = values.ndim - 3
    starts_full = (0,) * leading + tuple(starts)
    limits = tuple(values.shape[:leading]) + tuple((s + l for s, l in zip(starts, lengths)))
    return lax.slice(values, starts_full, limits)


def apply_operator(padded, potential):
    lengths = [padded.shape[i + 1] - 12 for i in range(3)]
    centre = window(padded, (6, 6, 6), lengths)
    summed = METRIC[0][0] * 0.0 * centre
    for d in range(3):
        second = SECOND[0] * centre
        for k in range(1, 7):
            forward = [6, 6, 6]
            forward[d] += k
            backward = [6, 6, 6]
            backward[d] -= k
            second = second + SECOND[k] * (
                window(padded, forward, lengths) + window(padded, backward, lengths)
            )
        summed = summed + METRIC[d][d] * second
    for d, e in ((0, 1), (0, 2), (1, 2)):
        widened = list(lengths)
        widened[d] += 12
        partial_sum = None
        for k in range(1, 7):
            forward = [6, 6, 6]
            forward[d] = 0
            forward[e] += k
            backward = [6, 6, 6]
            backward[d] = 0
            backward[e] -= k
            term = FIRST[k - 1] * (
                window(padded, forward, widened) - window(padded, backward, widened)
            )
            partial_sum = term if partial_sum is None else partial_sum + term
        crossed = None
        for k in range(1, 7):
            forward = [0, 0, 0]
            forward[d] = 6 + k
            backward = [0, 0, 0]
            backward[d] = 6 - k
            term = FIRST[k - 1] * (
                window(partial_sum, forward, lengths) - window(partial_sum, backward, lengths)
            )
            crossed = term if crossed is None else crossed + term
        summed = summed + 2.0 * METRIC[d][e] * crossed
    return -0.5 * summed + potential[None] * centre


def local(orbitals, potential):
    current = one_exchange(orbitals, ("gx", "gy"), ("gx", "gy"), (0, 0), (1, 2))
    previous = jnp.zeros_like(current)
    plane_x = gather_directly(potential, "gx", 0)
    plane = gather_directly(plane_x, "gy", 1)
    for degree_step in range(DEGREE):
        slab = extended(current, (("gz", 3),), 6)
        padded = jnp.pad(slab, ((0, 0), (6, 6), (6, 6), (0, 0)), mode="wrap")
        applied = apply_operator(padded, plane)
        factor = 1.0 if degree_step == 0 else 2.0
        carry_factor = 0.0 if degree_step == 0 else 1.0
        following = factor * (applied - CENTER * current) / HALF_WIDTH - carry_factor * previous
        previous = current
        current = following
    partly = lax.all_to_all(current, "gy", split_axis=2, concat_axis=0, tiled=True)
    current = lax.all_to_all(partly, "gx", split_axis=1, concat_axis=0, tiled=True)
    return current


def solution(mesh):
    return jax.shard_map(
        local,
        mesh=mesh,
        in_specs=(P(None, "gx", "gy", "gz"), P("gx", "gy", "gz")),
        out_specs=P(None, "gx", "gy", "gz"),
        check_vma=False,
    )
```

profile of v0, /device:TPU:24, one launch (start us, length us, event | category | flops | bytes accessed | tf_op | source)
XLA Modules:
  0.0 266.1 jit_solution(15221649158585164020)
XLA Ops:
  0.0 3.5 %copy.53 = f32[16,1,12,12,128]{4,1,3,2,0:T(1,128)} copy(f32[16,1,12,12,128]{4,0,3,2,1:T(8,128)} %bitcast.46) | data formatting | bytes 2359296 | tf_op jit(solution)/shard_map/reshape;reshape;reshape | solution.py:41
  3.5 5.9 %all-to-all-start = ((f32[16,1,12,12,128]{4,1,3,2,0:T(1,128)}), f32[16,1,12,12,128]{4,1,3,2,0:T(1,128)S(1)}, u32[]{:S(2)}, u32[]{:S(2)}) async-start(f32[16,1,12,12,128]{4,1,3,2,0:T(1,128)} %copy.53), calls=%async_computation | async-start | bytes 2359296 | tf_op jit(solution)/shard_map/all_to_all | solution.py:42
  9.4 0.0 copy-done.13
  9.4 17.8 %all-to-all-done = f32[16,1,12,12,128]{4,1,3,2,0:T(1,128)S(1)} async-done(((f32[16,1,12,12,128]{4,1,3,2,0:T(1,128)}), f32[16,1,12,12,128]{4,1,3,2,0:T(1,128)S(1)}, u32[]{:S(2)}, u32[]{:S(2)}) %all-to-all-start) | async-done | bytes 1179680 | tf_op jit(solution)/shard_map/all_to_all | solution.py:42
  27.2 0.8 broadcast_in_dim.6
  28.0 3.5 %all-to-all-start.1 = ((f32[4,12,12,128]{3,1,2,0:T(8,128)}), f32[4,12,12,128]{3,1,2,0:T(8,128)S(1)}, u32[]{:S(2)}, u32[]{:S(2)}) async-start(f32[4,12,12,128]{3,1,2,0:T(8,128)} %broadcast_in_dim.6), calls=%async_computation.1 | async-start | bytes 786432 | tf_op jit(solution)/shard_map/all_to_all | solution.py:49
  31.5 0.5 copy.54
  31.9 0.4 copy.55
  32.3 0.0 copy-start
  32.4 1.4 fusion.266
  33.8 1.8 copy.56
  35.5 3.3 %collective-permute-start = (f32[1,48,48,6]{2,1,3,0:T(8,128)S(1)}, f32[1,48,48,6]{2,1,3,0:T(8,128)S(1)}, u32[]{:S(2)}, u32[]{:S(2)}) collective-permute-start(f32[1,48,48,6]{2,1,3,0:T(8,128)S(1)} %copy.56), channel_id=1, source_target_pairs={{0,1},{1,2},{2,3},{3,4},{4,5},{5,6},{6,7},{7,0},{8,9},{9,10},{10,1... | collective-permute-start | bytes 165896 | tf_op jit(solution)/shard_map/ppermute | solution.py:63
  38.8 0.5 copy.57
  39.4 0.1 collective-permute-start.1
  39.4 0.1 all-to-all-done.1
  39.6 1.1 broadcast_in_dim.7
  40.7 4.5 %all-to-all-start.2 = ((f32[4,48,12,128]{3,1,2,0:T(8,128)}), f32[4,48,12,128]{3,1,2,0:T(8,128)}, u32[]{:S(2)}, u32[]{:S(2)}) async-start(f32[4,48,12,128]{3,1,2,0:T(8,128)} %broadcast_in_dim.7), calls=%async_computation.2 | async-start | bytes 2359296 | tf_op jit(solution)/shard_map/all_to_all | solution.py:49
  45.2 0.0 collective-permute-done
  45.2 0.6 copy.58
  45.8 0.0 copy-start.7
  45.8 2.4 collective-permute-done.1
  48.2 1.6 copy.59
  49.8 1.5 pad_maximum_fusion.15
  51.2 0.0 copy-done.7
  51.3 1.2 pad_maximum_fusion.4
  52.5 0.1 fusion.264
  52.5 4.6 %fusion.23 = f32[1,60,48,128]{3,1,2,0:T(8,128)S(1)} fusion(f32[1,60,48,140]{3,1,2,0:T(8,128)S(1)} %pad_maximum_fusion.4), kind=kLoop, calls=%fused_computation.88 | loop fusion | flops 6266880 | bytes 19169280 | tf_op jit(solution)/shard_map/add | solution.py:107
  57.2 4.4 %pad_maximum_fusion.6 = (f32[1,54,48,140]{3,1,2,0:T(8,128)}, f32[1,54,48,140]{3,1,2,0:T(8,128)}) fusion(f32[1,6,48,140]{3,1,2,0:T(8,128)S(1)} %get-tuple-element.18, f32[1,48,48,6]{3,1,2,0:T(8,128)S(1)} %copy-done.9, f32[1,48,48,128]{3,1,2,0:T(8,128)S(1)} %bitcast.37, f32[1,48,48,6]{3,1,2,0:T(8,128)S(1)} %copy-done.8, f32[1,6,48,140]{3,1,2,0:T(8,128)S(1)} %get-tuple-element.17), kind=kLoop, calls=%fused_computation.48 | loop fusion | flops 2177280 | bytes 4515840 | tf_op jit(solution)/shard_map/jit(_pad)/concatenate | solution.py:129
  61.6 3.1 %pad_maximum_fusion = f32[1,60,60,140]{3,1,2,0:T(8,128)S(1)} fusion(f32[1,60,6,140]{3,1,2,0:T(8,128)S(1)} %get-tuple-element.22, f32[1,6,48,140]{3,1,2,0:T(8,128)S(1)} %get-tuple-element.18, f32[1,48,48,6]{3,1,2,0:T(8,128)S(1)} %copy-done.9, f32[1,48,48,128]{3,1,2,0:T(8,128)S(1)} %bitcast.38, f32[1,48,48,6]{3,1,2,0:T(8,128)S(1)} %copy-done.8, ...), kind=kLoop, calls=%fused_computation.40 | loop fusion | flops 3024000 | bytes 4032000 | tf_op jit(solution)/shard_map/jit(_pad)/concatenate | solution.py:129
  64.8 4.8 %pad_maximum_fusion.2 = (f32[1,60,54,140]{3,1,2,0:T(8,128)S(1)}, f32[1,60,54,140]{3,1,2,0:T(8,128)S(1)}) fusion(f32[1,60,6,140]{3,1,2,0:T(8,128)} %copy-done.12, f32[1,6,48,140]{3,1,2,0:T(8,128)S(1)} %get-tuple-element.18, f32[1,48,48,6]{3,1,2,0:T(8,128)S(1)} %copy-done.10, f32[1,48,48,128]{3,1,2,0:T(8,128)S(1)} %bitcast.39, ...), kind=kLoop, calls=%fused_computation.42 | loop fusion | flops 4536000 | bytes 5644800 | tf_op jit(solution)/shard_map/jit(_pad)/concatenate | solution.py:129
  69.5 0.0 copy-start.2
  69.6 0.0 copy-start.3
  69.6 6.1 %fusion.34 = f32[1,60,48,128]{3,1,2,0:T(8,128)} fusion(f32[1,60,54,140]{3,1,2,0:T(8,128)S(1)} %get-tuple-element.10, f32[1,60,54,140]{3,1,2,0:T(8,128)S(1)} %get-tuple-element.9), kind=kLoop, calls=%fused_computation.105 | loop fusion | flops 6266880 | bytes 19169280 | tf_op jit(solution)/shard_map/add | solution.py:107
  75.7 0.0 copy-done.2
  75.7 4.3 %fusion.56 = f32[1,48,60,128]{3,1,2,0:T(8,128)S(1)} fusion(f32[1,60,60,140]{3,1,2,0:T(8,128)S(1)} %pad_maximum_fusion), kind=kLoop, calls=%fused_computation.139 | loop fusion | flops 6266880 | bytes 19169280 | tf_op jit(solution)/shard_map/add | solution.py:107
  80.0 0.0 all-to-all-done.2
  80.1 51.4 %broadcast_multiply_fusion = (f32[1,48,48,128]{3,1,2,0:T(8,128)S(1)}, f32[1,48,48,128]{3,1,2,0:T(8,128)}) fusion(f32[1,48,48,128]{3,1,2,0:T(8,128)} %bitcast.40, f32[1,48,60,128]{3,1,2,0:T(8,128)S(1)} %fusion.56, f32[1,60,48,128]{3,1,2,0:T(8,128)S(1)} %fusion.23, f32[1,60,48,128]{3,1,2,0:T(8,128)} %fusion.34, f32[1,48,48,6]{3,1,2,0:T(8,128)} %copy-done.7, ...), kind=kLoop, calls=%fused_computation.417 | loop fusion | flops 39518208 | bytes 75608064 | tf_op jit(solution)/shard_map/div | solution.py:133
  131.5 0.4 fusion.265
  131.9 0.6 copy-done.5
  132.5 0.5 copy.64
  133.1 3.2 %collective-permute-start.2 = (f32[1,48,48,6]{2,1,3,0:T(8,128)S(1)}, f32[1,48,48,6]{2,1,3,0:T(8,128)S(1)}, u32[]{:S(2)}, u32[]{:S(2)}) collective-permute-start(f32[1,48,48,6]{2,1,3,0:T(8,128)S(1)} %copy.64), channel_id=1, source_target_pairs={{0,1},{1,2},{2,3},{3,4},{4,5},{5,6},{6,7},{7,0},{8,9},{9,10},{10,1... | collective-permute-start | bytes 165896 | tf_op jit(solution)/shard_map/ppermute | solution.py:63
  136.3 1.2 copy.65
  137.5 0.0 collective-permute-start.3
  137.5 2.5 collective-permute-done.2
  140.0 0.6 copy.66
  140.6 6.6 %collective-permute-done.3 = f32[1,48,48,6]{2,1,3,0:T(8,128)S(1)} collective-permute-done((f32[1,48,48,6]{2,1,3,0:T(8,128)}, f32[1,48,48,6]{2,1,3,0:T(8,128)S(1)}, u32[]{:S(2)}, u32[]{:S(2)}) %collective-permute-start.3) | collective-permute-done | bytes 55328 | tf_op jit(solution)/shard_map/ppermute | solution.py:66
  147.3 1.5 copy.67
  148.8 1.5 pad_maximum_fusion.12
  150.3 0.0 copy-done.11
  150.3 1.2 pad_maximum_fusion.5
  151.5 0.1 fusion.263
  151.6 5.0 %fusion.1 = f32[1,60,48,128]{3,1,2,0:T(8,128)S(1)} fusion(f32[1,60,48,140]{3,1,2,0:T(8,128)S(1)} %pad_maximum_fusion.5), kind=kLoop, calls=%fused_computation.54 | loop fusion | flops 6266880 | bytes 19169280 | tf_op jit(solution)/shard_map/add | solution.py:107
  156.6 4.4 %pad_maximum_fusion.7 = (f32[1,54,48,140]{3,1,2,0:T(8,128)}, f32[1,54,48,140]{3,1,2,0:T(8,128)}) fusion(f32[1,6,48,140]{3,1,2,0:T(8,128)S(1)} %get-tuple-element.14, f32[1,48,48,6]{3,1,2,0:T(8,128)S(1)} %copy-done.11, f32[1,48,48,128]{3,1,2,0:T(8,128)S(1)} %copy-done.6, f32[1,48,48,6]{3,1,2,0:T(8,128)S(1)} %copy.66, f32[1,6,48,140]{3,1,2,0:T(8,128)S(1)} %get-tuple-element.13), kind=kLoop, calls=%fused_computation.50 | loop fusion | flops 2177280 | bytes 4515840 | tf_op jit(solution)/shard_map/jit(_pad)/concatenate | solution.py:129
  161.0 3.1 %pad_maximum_fusion.1 = f32[1,60,60,140]{3,1,2,0:T(8,128)S(1)} fusion(f32[1,60,6,140]{3,1,2,0:T(8,128)S(1)} %get-tuple-element.20, f32[1,6,48,140]{3,1,2,0:T(8,128)S(1)} %get-tuple-element.14, f32[1,48,48,6]{3,1,2,0:T(8,128)S(1)} %copy-done.11, f32[1,48,48,128]{3,1,2,0:T(8,128)S(1)} %copy-done.6, f32[1,48,48,6]{3,1,2,0:T(8,128)S(1)} %copy.66, ...), kind=kLoop, calls=%fused_computation.41 | loop fusion | flops 3024000 | bytes 4032000 | tf_op jit(solution)/shard_map/jit(_pad)/concatenate | solution.py:129
  164.2 5.9 %pad_maximum_fusion.3 = (f32[1,60,54,140]{3,1,2,0:T(8,128)S(1)}, f32[1,60,54,140]{3,1,2,0:T(8,128)}) fusion(f32[1,60,6,140]{3,1,2,0:T(8,128)S(1)} %get-tuple-element.20, f32[1,6,48,140]{3,1,2,0:T(8,128)S(1)} %get-tuple-element.14, f32[1,48,48,6]{3,1,2,0:T(8,128)S(1)} %copy-done.11, f32[1,48,48,128]{3,1,2,0:T(8,128)S(1)} %copy-done.6, ...), kind=kLoop, calls=%fused_computation.44 | loop fusion | flops 4536000 | bytes 5644800 | tf_op jit(solution)/shard_map/jit(_pad)/concatenate | solution.py:129
  170.1 4.3 %fusion.45 = f32[1,48,60,128]{3,1,2,0:T(8,128)S(1)} fusion(f32[1,60,60,140]{3,1,2,0:T(8,128)S(1)} %pad_maximum_fusion.1), kind=kLoop, calls=%fused_computation.122 | loop fusion | flops 6266880 | bytes 19169280 | tf_op jit(solution)/shard_map/add | solution.py:107
  174.4 0.0 copy-start.1
  174.5 10.8 %fusion.12 = f32[1,60,48,128]{3,1,2,0:T(8,128)S(1)} fusion(f32[1,60,54,140]{3,1,2,0:T(8,128)} %get-tuple-element.8, f32[1,60,54,140]{3,1,2,0:T(8,128)S(1)} %get-tuple-element.7), kind=kLoop, calls=%fused_computation.71 | loop fusion | flops 6266880 | bytes 19169280 | tf_op jit(solution)/shard_map/add | solution.py:107
  185.3 0.0 copy-done.1
  185.3 38.5 %fusion.261 = f32[1,48,48,128]{3,1,0,2:T(8,128)} fusion(f32[1,48,48,128]{3,1,2,0:T(8,128)S(1)} %bitcast.41, f32[1,48,48,128]{3,1,2,0:T(8,128)} %get-tuple-element.6, f32[1,48,48,128]{3,1,2,0:T(8,128)S(1)} %copy-done.6, f32[1,48,60,128]{3,1,2,0:T(8,128)S(1)} %fusion.45, f32[1,60,48,128]{3,1,2,0:T(8,128)S(1)} %fusion.1, f32[1,60,48,128]{3,1,2,0:T(8,128)S(1)} %fusion.12, ...), kind=kLoop, calls=%fused_computation.416 | loop fusion | flops 39813120 | bytes 76787712 | tf_op jit(solution)/shard_map/sub | solution.py:133
  223.8 19.3 %all_to_all.51 = f32[1,48,48,128]{3,1,0,2:T(8,128)S(1)} all-to-all(f32[1,48,48,128]{3,1,0,2:T(8,128)} %fusion.261), channel_id=1, replica_groups=mesh['gx'=4,'gy'=4,'gz'=8] {'gy'}, dimensions={2} | all-to-all | bytes 2359296 | tf_op jit(solution)/shard_map/all_to_all | solution.py:136
  243.1 0.8 copy.71
  243.9 20.7 %all_to_all.52 = f32[4,48,12,128]{3,0,2,1:T(4,128)S(1)} all-to-all(f32[4,48,12,128]{3,0,2,1:T(4,128)S(1)} %copy.71), channel_id=1, replica_groups=mesh['gx'=4,'gy'=4,'gz'=8] {'gx'}, dimensions={1} | all-to-all | bytes 2359296 | tf_op jit(solution)/shard_map/all_to_all | solution.py:137
  264.6 1.3 copy.72
  (20 shorter events, 0.1 us)
Async XLA Ops:
  3.5 5.9 %copy-start.13 = (f32[12,12,128]{2,1,0:T(8,128)S(1)}, f32[12,12,128]{2,1,0:T(8,128)}, u32[]{:S(2)}) copy-start(f32[12,12,128]{2,1,0:T(8,128)} %param.3) | copy-start | bytes 221188
  3.5 23.7 %all-to-all-start = ((f32[16,1,12,12,128]{4,1,3,2,0:T(1,128)}), f32[16,1,12,12,128]{4,1,3,2,0:T(1,128)S(1)}, u32[]{:S(2)}, u32[]{:S(2)}) async-start(f32[16,1,12,12,128]{4,1,3,2,0:T(1,128)} %copy.53), calls=%async_computation | async-start | bytes 2359296 | tf_op jit(solution)/shard_map/all_to_all | solution.py:42
  28.0 11.5 %all-to-all-start.1 = ((f32[4,12,12,128]{3,1,2,0:T(8,128)}), f32[4,12,12,128]{3,1,2,0:T(8,128)S(1)}, u32[]{:S(2)}, u32[]{:S(2)}) async-start(f32[4,12,12,128]{3,1,2,0:T(8,128)} %broadcast_in_dim.6), calls=%async_computation.1 | async-start | bytes 786432 | tf_op jit(solution)/shard_map/all_to_all | solution.py:49
  32.3 32.4 %copy-start = (f32[1,48,4,12,128]{4,1,3,2,0:T(8,128)}, f32[1,48,4,12,128]{4,1,3,2,0:T(8,128)S(1)}, u32[]{:S(2)}) copy-start(f32[1,48,4,12,128]{4,1,3,2,0:T(8,128)S(1)} %copy.55) | copy-start | bytes 3538948
  35.5 9.6 %collective-permute-start = (f32[1,48,48,6]{2,1,3,0:T(8,128)S(1)}, f32[1,48,48,6]{2,1,3,0:T(8,128)S(1)}, u32[]{:S(2)}, u32[]{:S(2)}) collective-permute-start(f32[1,48,48,6]{2,1,3,0:T(8,128)S(1)} %copy.56), channel_id=1, source_target_pairs={{0,1},{1,2},{2,3},{3,4},{4,5},{5,6},{6,7},{7,0},{8,9},{9,10},{10,1... | collective-permute-start | bytes 165896 | tf_op jit(solution)/shard_map/ppermute | solution.py:63
  39.4 8.8 %collective-permute-start.1 = (f32[1,48,48,6]{2,1,3,0:T(8,128)S(1)}, f32[1,48,48,6]{2,1,3,0:T(8,128)S(1)}, u32[]{:S(2)}, u32[]{:S(2)}) collective-permute-start(f32[1,48,48,6]{2,1,3,0:T(8,128)S(1)} %copy.57), channel_id=1, source_target_pairs={{1,0},{2,1},{3,2},{4,3},{5,4},{6,5},{7,6},{0,7},{9,8},{10,9},{11,1... | collective-permute-start | bytes 165896 | tf_op jit(solution)/shard_map/ppermute | solution.py:66
  40.7 39.4 %all-to-all-start.2 = ((f32[4,48,12,128]{3,1,2,0:T(8,128)}), f32[4,48,12,128]{3,1,2,0:T(8,128)}, u32[]{:S(2)}, u32[]{:S(2)}) async-start(f32[4,48,12,128]{3,1,2,0:T(8,128)} %broadcast_in_dim.7), calls=%async_computation.2 | async-start | bytes 2359296 | tf_op jit(solution)/shard_map/all_to_all | solution.py:49
  45.8 5.5 %copy-start.7 = (f32[1,48,48,6]{3,1,2,0:T(8,128)}, f32[1,48,48,6]{3,1,2,0:T(8,128)S(1)}, u32[]{:S(2)}) copy-start(f32[1,48,48,6]{3,1,2,0:T(8,128)S(1)} %copy.58) | copy-start | bytes 165892
  49.8 1.5 copy-start.9
  52.5 9.1 %copy-start.12 = (f32[1,60,6,140]{3,1,2,0:T(8,128)}, f32[1,60,6,140]{3,1,2,0:T(8,128)S(1)}, u32[]{:S(2)}) copy-start(f32[1,60,6,140]{3,1,2,0:T(8,128)S(1)} %get-tuple-element.22) | copy-start | bytes 604804
  52.5 4.6 %copy-start.8 = (f32[1,48,48,6]{3,1,2,0:T(8,128)S(1)}, f32[1,48,48,6]{3,1,2,0:T(8,128)}, u32[]{:S(2)}) copy-start(f32[1,48,48,6]{3,1,2,0:T(8,128)} %copy-done.7) | copy-start | bytes 165892
  61.6 3.1 %copy-start.10 = (f32[1,48,48,6]{3,1,2,0:T(8,128)S(1)}, f32[1,48,48,6]{3,1,2,0:T(8,128)}, u32[]{:S(2)}) copy-start(f32[1,48,48,6]{3,1,2,0:T(8,128)} %copy.59) | copy-start | bytes 165892
  69.5 6.2 %copy-start.2 = (f32[1,60,54,140]{3,1,2,0:T(8,128)}, f32[1,60,54,140]{3,1,2,0:T(8,128)S(1)}, u32[]{:S(2)}) copy-start(f32[1,60,54,140]{3,1,2,0:T(8,128)S(1)} %get-tuple-element.9) | copy-start | bytes 5443204
  69.6 6.2 %copy-start.3 = (f32[1,60,54,140]{3,1,2,0:T(8,128)}, f32[1,60,54,140]{3,1,2,0:T(8,128)S(1)}, u32[]{:S(2)}) copy-start(f32[1,60,54,140]{3,1,2,0:T(8,128)S(1)} %get-tuple-element.10) | copy-start | bytes 5443204
  131.5 1.0 copy-start.5
  133.1 7.0 %collective-permute-start.2 = (f32[1,48,48,6]{2,1,3,0:T(8,128)S(1)}, f32[1,48,48,6]{2,1,3,0:T(8,128)S(1)}, u32[]{:S(2)}, u32[]{:S(2)}) collective-permute-start(f32[1,48,48,6]{2,1,3,0:T(8,128)S(1)} %copy.64), channel_id=1, source_target_pairs={{0,1},{1,2},{2,3},{3,4},{4,5},{5,6},{6,7},{7,0},{8,9},{9,10},{10,1... | collective-permute-start | bytes 165896 | tf_op jit(solution)/shard_map/ppermute | solution.py:63
  137.5 11.3 %copy-start.6 = (f32[1,48,48,128]{3,1,2,0:T(8,128)S(1)}, f32[1,48,48,128]{3,1,2,0:T(8,128)}, u32[]{:S(2)}) copy-start(f32[1,48,48,128]{3,1,2,0:T(8,128)} %copy-done.5) | copy-start | bytes 3538948
  137.5 9.8 %collective-permute-start.3 = (f32[1,48,48,6]{2,1,3,0:T(8,128)}, f32[1,48,48,6]{2,1,3,0:T(8,128)S(1)}, u32[]{:S(2)}, u32[]{:S(2)}) collective-permute-start(f32[1,48,48,6]{2,1,3,0:T(8,128)} %copy.65), channel_id=1, source_target_pairs={{1,0},{2,1},{3,2},{4,3},{5,4},{6,5},{7,6},{0,7},{9,8},{10,9},{11,1... | collective-permute-start | bytes 165896 | tf_op jit(solution)/shard_map/ppermute | solution.py:66
  148.8 1.5 copy-start.11
  170.1 4.3 %copy-start.4 = (f32[1,60,54,140]{3,1,2,0:T(8,128)}, f32[1,60,54,140]{3,1,2,0:T(8,128)S(1)}, u32[]{:S(2)}) copy-start(f32[1,60,54,140]{3,1,2,0:T(8,128)S(1)} %get-tuple-element.7) | copy-start | bytes 5443204
  174.4 10.8 %copy-start.1 = (f32[1,48,4,12,128]{4,1,3,2,0:T(8,128)S(1)}, f32[1,48,4,12,128]{4,1,3,2,0:T(8,128)}, u32[]{:S(2)}) copy-start(f32[1,48,4,12,128]{4,1,3,2,0:T(8,128)} %copy-done) | copy-start | bytes 3538948
where the time goes:
time: 271 us; the launch traced here: 266 us
  other arithmetic  156 us (58%)
  blocking collectives  40 us (15%)
  waiting for transfers between devices  29.4 us (11%)
  starting transfers between devices  20.4 us (8%)
  local copies, waits for them, and re-layouts  19.3 us (7%)
    div x1, other arithmetic, local(): factor * (applied - CENTER * current) / HALF_WIDTH - carry_factor * previous  51.4 us
    sub x1, other arithmetic, local(): factor * (applied - CENTER * current) / HALF_WIDTH - carry_factor * previous  38.5 us
    add x6, other arithmetic, apply_operator(): partial_sum = term if partial_sum is None else partial_sum + term  35.3 us
    concatenate x8, other arithmetic, local(): padded = jnp.pad(slab, ((0, 0), (6, 6), (6, 6), (0, 0)), mode='wrap')  28.2 us
    all_to_all x1, blocking collectives, local(): lax.all_to_all(partly, 'gx', split_axis=1, concat_axis=0, tiled=True)  20.7 us
    all_to_all x1, blocking collectives, local(): lax.all_to_all(current, 'gy', split_axis=2, concat_axis=0, tiled=True)  19.3 us
    all_to_all x1, waiting for transfers between devices, one_exchange(): lax.all_to_all(blocks, axis, split_axis=0, concat_axis=0, tiled=True)  17.8 us
    ppermute x2, waiting for transfers between devices, extended(): lax.ppermute(lax.slice_in_dim(block, 0, width, axis=dim), axis, backward)  8.98 us
  transfers between devices with their start and end apart: 7, of which 5 were waited for; matrix products, arithmetic and copies ran while one was open for 15% of the time, Pallas kernels for 0%

commit v1 on v0

v1 whole, which is shorter than its diff:
```python
import functools

import jax
import jax.numpy as jnp
import numpy as np
from jax import lax
from jax.experimental import pallas as pl
from jax.experimental.pallas import tpu as pltpu
from jax.sharding import PartitionSpec as P

MESH = pl.DeviceIdType.MESH
SECOND = (
    -5369.0 / 1800.0,
    12.0 / 7.0,
    -15.0 / 56.0,
    10.0 / 189.0,
    -1.0 / 112.0,
    2.0 / 1925.0,
    -1.0 / 16632.0,
)
FIRST = (6.0 / 7.0, -15.0 / 56.0, 5.0 / 63.0, -1.0 / 56.0, 3.0 / 385.0, -1.0 / 792.0)
G01, G02, G12 = 0.25, 0.15, 0.2
CENTER = 10.5
HALF_WIDTH = 9.5
SIGMA = -0.5 / HALF_WIDTH

XC = [SIGMA * c for c in SECOND]
XA = [SIGMA * 2.0 * G02 * a for a in FIRST]

F32 = jnp.float32
BF16 = jnp.bfloat16
STRIDE = 16
ROWS = 12 * STRIDE


def order_of_rows():
    rows = []
    for s in range(4):
        rows += [12 * s + r for r in range(8)]
    for s in range(4):
        rows += [12 * s + 8 + r for r in range(4)]
    return rows


def two_parts(m):
    hi = m.astype(np.float32).astype(jnp.bfloat16)
    lo = (m - hi.astype(np.float64)).astype(np.float32).astype(jnp.bfloat16)
    return hi, lo


def z_matrices():
    m = np.zeros((140, 256))
    for z in range(128):
        for k in range(1, 7):
            m[z + 6 + k, z] += FIRST[k - 1]
            m[z + 6 - k, z] -= FIRST[k - 1]
            m[z + 6 + k, 128 + z] += SIGMA * SECOND[k]
            m[z + 6 - k, 128 + z] += SIGMA * SECOND[k]
    inside = m[6:134]
    halo = np.zeros((128, 256))
    halo[122:128] = m[0:6]
    halo[0:6] = m[134:140]
    i1, i2 = two_parts(inside)
    h1, h2 = two_parts(halo)
    return np.stack([np.concatenate([i1, i1]), np.concatenate([i2, h1]), np.concatenate([h2, h1])])


def y_matrices():
    rows = order_of_rows()
    place = {y: r for r, y in enumerate(rows)}
    d1 = np.zeros((48, 48))
    d2 = np.zeros((48, 48))
    for y in range(48):
        for k in range(1, 7):
            d1[place[y], place[(y + k) % 48]] += FIRST[k - 1]
            d1[place[y], place[(y - k) % 48]] -= FIRST[k - 1]
            d2[place[y], place[(y + k) % 48]] += SECOND[k]
            d2[place[y], place[(y - k) % 48]] += SECOND[k]
    a1, a2 = two_parts(np.concatenate([(G01 / G02) * d1, SIGMA * d2]))
    b1, b2 = two_parts(SIGMA * 2.0 * G12 * d1)
    return np.concatenate([a1, a1, a2], axis=1), np.concatenate([b1, b1, b2], axis=1)


def split(value):
    hi = value.astype(BF16)
    lo = (value - hi.astype(F32)).astype(BF16)
    return hi, lo


def kernel(
    orb,
    pot,
    mz,
    my1,
    my2,
    out,
    sm,
    sr,
    spm,
    spr,
    v,
    rr,
    vp,
    rp,
    zs,
    zr,
    cs,
    cr,
    part,
    wf,
    v1,
    v2,
    h1,
    h2,
    tz,
    yf,
    ro,
    om,
    orr,
    tin_s,
    tin_r,
    zx_s,
    zx_r,
    xc_s,
    xc_r,
    to_s,
    to_r,
):
    gx = lax.axis_index("gx")
    gy = lax.axis_index("gy")
    gz = lax.axis_index("gz")
    x_at = [{"gx": lax.rem(gx + 3, 4)}, {"gx": lax.rem(gx + 1, 4)}]
    z_at = [{"gz": lax.rem(gz + 7, 8)}, {"gz": lax.rem(gz + 1, 8)}]
    y_of = [lax.rem(gy + d, 4) for d in range(4)]

    def copy(src, dst, send, recv, device):
        return pltpu.make_async_remote_copy(
            src_ref=src, dst_ref=dst, send_sem=send, recv_sem=recv, device_id=device, device_id_type=MESH
        )

    barrier = pltpu.get_barrier_semaphore()
    for device in x_at + z_at + [{"gy": y_of[d]} for d in range(1, 4)]:
        pl.semaphore_signal(barrier, inc=1, device_id=device, device_id_type=MESH)

    low_half = lax.broadcasted_iota(jnp.int32, (8, 128), 0) < 4
    lane = lax.broadcasted_iota(jnp.int32, (48, 128), 1)

    def pair(a, b):
        return (
            jnp.where(low_half, a, pltpu.roll(b, 4, 0)),
            jnp.where(low_half, pltpu.roll(a, 4, 0), b),
        )

    started = []

    def start(c):
        c.start()
        started.append(c)

    def tin(c, d):
        to = {"gy": y_of[d]}
        if c == 4:
            return [
                copy(spm, vp.at[:, gy], tin_s.at[c, d, 0], tin_r.at[c, d, 0], to),
                copy(spr, rp.at[gy], tin_s.at[c, d, 1], tin_r.at[c, d, 1], to),
            ]
        return [
            copy(sm.at[c, y_of[d]], v.at[c, 0, :, gy], tin_s.at[c, d, 0], tin_r.at[c, d, 0], to),
            copy(sr.at[c, y_of[d]], rr.at[c, gy], tin_s.at[c, d, 1], tin_r.at[c, d, 1], to),
        ]

    def prepare(c):
        if c == 4:
            for x in range(12):
                spm[x] = pot[x, 0:8]
            for p in range(6):
                spr[p] = jnp.concatenate([pot[2 * p, 8:12], pot[2 * p + 1, 8:12]], axis=0)
            return

        def band(g, carry):
            b = 4 * c + g
            for x in range(12):
                sm[c, g, x] = orb[pl.ds(x * ROWS + b, 8, stride=STRIDE), :]
            for p in range(6):
                lo = orb[pl.ds(2 * p * ROWS + 8 * STRIDE + b, 4, stride=STRIDE), :]
                hi = orb[pl.ds((2 * p + 1) * ROWS + 8 * STRIDE + b, 4, stride=STRIDE), :]
                sr[c, g, p] = jnp.concatenate([lo, hi], axis=0)
            return carry

        lax.fori_loop(0, 4, band, 0)

    def keep_own(c):
        if c == 4:
            vp[:, gy] = spm[...]
            rp[gy] = spr[...]
        else:
            v[c, 0, :, gy] = sm[c, gy]
            rr[c, gy] = sr[c, gy]

    def assemble(rest, dest):
        for p in range(6):
            for t in range(2):
                even, odd = pair(rest[2 * t, p], rest[2 * t + 1, p])
                dest(2 * p, 4 + t, even)
                dest(2 * p + 1, 4 + t, odd)

    def zx(c, step, side):
        return copy(
            zs.at[c, step, side], zr.at[c, step, 1 - side], zx_s.at[c, step, side], zx_r.at[c, step, side], z_at[side]
        )

    def edges(c, step):
        low = None
        high = None
        for x in range(12):
            val = v[c, step, x].reshape(48, 128)
            a = val if x == 0 else pltpu.roll(val, 6 * x, 1)
            b = pltpu.roll(val, 6 * x + 6, 1)
            low = a if x == 0 else jnp.where(lane >= 6 * x, a, low)
            high = b if x == 0 else jnp.where(lane >= 6 * x, b, high)
        zs[c, step, 0] = low.reshape(6, 8, 128)
        zs[c, step, 1] = high.reshape(6, 8, 128)
        for side in range(2):
            start(zx(c, step, side))

    def stage_a(c):
        for d in range(1, 4):
            for one in tin(c, d):
                one.wait_recv()

        def dest(x, t, value):
            v[c, 0, x, t] = value

        assemble(rr.at[c], dest)
        edges(c, 0)

    def xc(c, step, side):
        return copy(
            cs.at[c, step, side], cr.at[c, step, side], xc_s.at[c, step, side], xc_r.at[c, step, side], x_at[side]
        )

    def stage_b(c, step):
        for x in range(12):
            a, b = split(v[c, step, x].reshape(48, 128))
            v1[x] = a
            v2[x] = b
        for side in range(2):
            zx(c, step, side).wait_recv()
        below = zr[c, step, 0].reshape(48, 128)
        above = zr[c, step, 1].reshape(48, 128)
        for x in range(12):
            up = above if x == 0 else pltpu.roll(above, 128 - 6 * x, 1)
            down = pltpu.roll(below, 122 - 6 * x, 1)
            h = jnp.where(lane < 6, up, jnp.where(lane >= 122, down, 0.0))
            a, b = split(h)
            h1[x] = a
            h2[x] = b
        f1 = v1[...].reshape(576, 128)
        f2 = v2[...].reshape(576, 128)
        g1 = h1[...].reshape(576, 128)
        g2 = h2[...].reshape(576, 128)
        acc = jnp.dot(jnp.concatenate([f1, f2], axis=1), mz[0], preferred_element_type=F32)
        acc += jnp.dot(jnp.concatenate([f1, g1], axis=1), mz[1], preferred_element_type=F32)
        acc += jnp.dot(jnp.concatenate([g1, g2], axis=1), mz[2], preferred_element_type=F32)
        tz[...] = acc
        for xp in range(6):
            x0, x1 = 2 * xp, 2 * xp + 1
            a = jnp.concatenate([v1[x0], v1[x1]], axis=1)
            b = jnp.concatenate([v2[x0], v2[x1]], axis=1)
            q = jnp.dot(my1[...], jnp.concatenate([a, b, a], axis=0), preferred_element_type=F32)
            t = jnp.concatenate([tz[48 * x0 : 48 * x0 + 48, 0:128], tz[48 * x1 : 48 * x1 + 48, 0:128]], axis=1)
            s = jnp.concatenate([tz[48 * x0 : 48 * x0 + 48, 128:256], tz[48 * x1 : 48 * x1 + 48, 128:256]], axis=1)
            ta, tb = split(t)
            r = jnp.dot(my2[...], jnp.concatenate([ta, tb, ta], axis=0), preferred_element_type=F32)
            w = q[0:48] + t
            r = r + q[48:96] + s
            for i, x in enumerate((x0, x1)):
                wf[x] = w[:, 128 * i : 128 * i + 128].reshape(6, 8, 128)
                part[c, x] = r[:, 128 * i : 128 * i + 128].reshape(6, 8, 128)

        def tile(t, carry):
            acc = [None] * 24
            for half in range(2):
                for j in range(6 * half, 6 * half + 6):
                    vj = v[c, step, j, t]
                    wj = wf[j, t]
                    for k in range(1, 7):
                        cv = XC[k] * vj
                        aw = XA[k - 1] * wj
                        lo, hi = j + 6 - k, j + 6 + k
                        acc[lo] = cv + aw if acc[lo] is None else acc[lo] + (cv + aw)
                        acc[hi] = cv - aw if acc[hi] is None else acc[hi] + (cv - aw)
            for i in range(6):
                cs[c, step, 0, i, t] = acc[i]
                cs[c, step, 1, i, t] = acc[18 + i]
            for i in range(12):
                part[c, i, t] = part[c, i, t] + acc[6 + i]
            return carry

        lax.fori_loop(0, 6, tile, 0)
        for side in range(2):
            start(xc(c, step, side))

    def to(c, d):
        at = {"gy": y_of[d]}
        return [
            copy(yf.at[c, :, y_of[d]], om.at[c, gy], to_s.at[c, d, 0], to_r.at[c, d, 0], at),
            copy(ro.at[c, y_of[d]], orr.at[c, gy], to_s.at[c, d, 1], to_r.at[c, d, 1], at),
        ]

    def stage_c(c, step):
        for side in range(2):
            xc(c, step, side).wait_recv()
        for x in range(12):
            got = cr[c, step, 1, x] if x < 6 else cr[c, step, 0, x - 6]
            y = part[c, x] + got + vp[x] * v[c, step, x]
            if step == 0:
                v[c, 1, x] = y
            else:
                yf[c, x] = 2.0 * y - v[c, 0, x]
        if step == 0:
            edges(c, 1)
            return
        for p in range(6):
            for t in range(2):
                even, odd = pair(yf[c, 2 * p, 4 + t], yf[c, 2 * p + 1, 4 + t])
                ro[c, 2 * t, p] = even
                ro[c, 2 * t + 1, p] = odd
        for d in range(1, 4):
            for one in to(c, d):
                start(one)
        om[c, gy] = yf[c, :, gy]
        orr[c, gy] = ro[c, gy]

    def stage_d(c):
        for d in range(1, 4):
            for one in to(c, d):
                one.wait_recv()

        def band(g, carry):
            b = 4 * c + g
            for x in range(12):
                out[pl.ds(x * ROWS + b, 8, stride=STRIDE), :] = om[c, g, x]
            for p in range(6):
                r = orr[c, g, p]
                out[pl.ds(2 * p * ROWS + 8 * STRIDE + b, 4, stride=STRIDE), :] = r[0:4]
                out[pl.ds((2 * p + 1) * ROWS + 8 * STRIDE + b, 4, stride=STRIDE), :] = r[4:8]
            return carry

        lax.fori_loop(0, 4, band, 0)

    def send_in(c):
        for d in (2, 1, 3):
            for one in tin(c, d):
                start(one)
        keep_own(c)

    prepare(0)
    pl.semaphore_wait(barrier, 7)
    send_in(0)
    for c in (1, 2, 4, 3):
        prepare(c)
        send_in(c)

    stage_a(0)
    stage_a(1)
    stage_b(0, 0)
    stage_a(2)
    stage_b(1, 0)
    for d in range(1, 4):
        for one in tin(4, d):
            one.wait_recv()

    def place(x, t, value):
        vp[x, t] = value

    assemble(rp, place)
    for x in range(12):
        vp[x] = (vp[x] - CENTER) * (1.0 / HALF_WIDTH) + 3.0 * XC[0]
    stage_a(3)
    stage_b(2, 0)
    stage_c(0, 0)
    stage_b(3, 0)
    stage_c(1, 0)
    stage_b(0, 1)
    stage_c(2, 0)
    stage_b(1, 1)
    stage_c(3, 0)
    stage_b(2, 1)
    stage_c(0, 1)
    stage_b(3, 1)
    stage_c(1, 1)
    stage_c(2, 1)
    stage_d(0)
    stage_c(3, 1)
    stage_d(1)
    stage_d(2)
    stage_d(3)
    for one in started:
        one.wait_send()


def local(orbitals, potential):
    rows = jnp.transpose(orbitals, (1, 2, 0, 3)).reshape(2304, 128)
    my1, my2 = y_matrices()
    vmem = pl.BlockSpec(memory_space=pltpu.VMEM)
    tile = (6, 8, 128)
    slab = (12, *tile)
    sem = pltpu.SemaphoreType.DMA
    out = pl.pallas_call(
        kernel,
        out_shape=jax.ShapeDtypeStruct((2304, 128), F32),
        in_specs=[vmem] * 5,
        out_specs=vmem,
        scratch_shapes=[
            pltpu.VMEM((4, 4, 12, 8, 128), F32),
            pltpu.VMEM((4, 4, *tile), F32),
            pltpu.VMEM((12, 8, 128), F32),
            pltpu.VMEM(tile, F32),
            pltpu.VMEM((4, 2, *slab), F32),
            pltpu.VMEM((4, 4, *tile), F32),
            pltpu.VMEM(slab, F32),
            pltpu.VMEM((4, *tile), F32),
            pltpu.VMEM((4, 2, 2, *tile), F32),
            pltpu.VMEM((4, 2, 2, *tile), F32),
            pltpu.VMEM((4, 2, 2, 6, *tile), F32),
            pltpu.VMEM((4, 2, 2, 6, *tile), F32),
            pltpu.VMEM((4, *slab), F32),
            pltpu.VMEM(slab, F32),
            pltpu.VMEM((12, 48, 128), BF16),
            pltpu.VMEM((12, 48, 128), BF16),
            pltpu.VMEM((12, 48, 128), BF16),
            pltpu.VMEM((12, 48, 128), BF16),
            pltpu.VMEM((576, 256), F32),
            pltpu.VMEM((4, *slab), F32),
            pltpu.VMEM((4, 4, *tile), F32),
            pltpu.VMEM((4, 4, 12, 8, 128), F32),
            pltpu.VMEM((4, 4, *tile), F32),
            sem((5, 4, 2)),
            sem((5, 4, 2)),
            sem((4, 2, 2)),
            sem((4, 2, 2)),
            sem((4, 2, 2)),
            sem((4, 2, 2)),
            sem((4, 4, 2)),
            sem((4, 4, 2)),
        ],
        compiler_params=pltpu.CompilerParams(
            collective_id=0, has_side_effects=True, vmem_limit_bytes=60 * 1024 * 1024
        ),
    )(rows, potential, jnp.asarray(z_matrices()), jnp.asarray(my1), jnp.asarray(my2))
    return jnp.transpose(out.reshape(12, 12, 16, 128), (2, 0, 1, 3))


def solution(mesh):
    return jax.shard_map(
        local,
        mesh=mesh,
        in_specs=(P(None, "gx", "gy", "gz"), P("gx", "gy", "gz")),
        out_specs=P(None, "gx", "gy", "gz"),
        check_vma=False,
    )
```

time: 271 us -> 62.7 us (0.23)
  the two profiles are of different devices: /device:TPU:24 before, /device:TPU:1 now
where the time goes in v1:
time: 62.7 us; the launch traced here: 62.6 us
  Pallas kernels  60.2 us (96%)
  local copies, waits for them, and re-layouts  2.36 us (4%)
    pallas_call x1, Pallas kernels, local(): pl.pallas_call(kernel, out_shape=jax.ShapeDtypeStruct((2304, 128), F32),...  60.2 us
    unnamed x1, local copies, waits for them, and re-layouts  2.36 us

profile of v1, /device:TPU:1, one launch (start us, length us, event | category | flops | bytes accessed | tf_op | source)
XLA Modules:
  0.0 62.6 jit_solution(4571721328537766275)
XLA Ops:
  0.0 60.2 %shard_map.55 = f32[2304,128]{1,0:T(8,128)} custom-call(f32[2304,128]{1,0:T(8,128)} %bitcast.7, f32[12,12,128]{2,1,0:T(8,128)} %pot.1, bf16[3,256,256]{2,1,0:T(8,128)(2,1)} %constant.6.clone.mz, bf16[96,144]{1,0:T(8,128)(2,1)} %constant.7.clone.my1, bf16[48,144]{1,0:T(8,128)(2,1)} %constant.8.clone.my2), custom_call_target="tpu_custom_call" | custom-call | tf_op jit(solution)/shard_map/pallas_call | solution.py:410
  60.2 2.4 %copy.7 = f32[16,12,12,128]{3,0,2,1:T(8,128)} copy(f32[16,12,12,128]{3,0,2,1:T(8,128)} %bitcast.6) | data formatting | bytes 2359296

commit v2 on v1

v2 whole, which is shorter than its diff:
```python
import functools

import jax
import jax.numpy as jnp
import numpy as np
from jax import lax
from jax.experimental import pallas as pl
from jax.experimental.pallas import tpu as pltpu
from jax.sharding import PartitionSpec as P

MESH = pl.DeviceIdType.MESH
SECOND = (
    -5369.0 / 1800.0,
    12.0 / 7.0,
    -15.0 / 56.0,
    10.0 / 189.0,
    -1.0 / 112.0,
    2.0 / 1925.0,
    -1.0 / 16632.0,
)
FIRST = (6.0 / 7.0, -15.0 / 56.0, 5.0 / 63.0, -1.0 / 56.0, 3.0 / 385.0, -1.0 / 792.0)
G01, G02, G12 = 0.25, 0.15, 0.2
CENTER = 10.5
HALF_WIDTH = 9.5
SIGMA = -0.5 / HALF_WIDTH

XC = [SIGMA * c for c in SECOND]
XA = [SIGMA * 2.0 * G02 * a for a in FIRST]

F32 = jnp.float32
BF16 = jnp.bfloat16
STRIDE = 8
ROWS = 12 * STRIDE


def order_of_rows():
    rows = []
    for s in range(4):
        rows += [12 * s + r for r in range(8)]
    for s in range(4):
        rows += [12 * s + 8 + r for r in range(4)]
    return rows


def two_parts(m):
    hi = m.astype(np.float32).astype(jnp.bfloat16)
    lo = (m - hi.astype(np.float64)).astype(np.float32).astype(jnp.bfloat16)
    return hi, lo


def z_matrices():
    m = np.zeros((140, 256))
    for z in range(128):
        for k in range(1, 7):
            m[z + 6 + k, z] += FIRST[k - 1]
            m[z + 6 - k, z] -= FIRST[k - 1]
            m[z + 6 + k, 128 + z] += SIGMA * SECOND[k]
            m[z + 6 - k, 128 + z] += SIGMA * SECOND[k]
    inside = m[6:134]
    halo = np.zeros((128, 256))
    halo[122:128] = m[0:6]
    halo[0:6] = m[134:140]
    i1, i2 = two_parts(inside)
    h1, h2 = two_parts(halo)
    return np.stack([np.concatenate([i1, i1]), np.concatenate([i2, h1]), np.concatenate([h2, h1])])


def y_matrices():
    rows = order_of_rows()
    place = {y: r for r, y in enumerate(rows)}
    d1 = np.zeros((48, 48))
    d2 = np.zeros((48, 48))
    for y in range(48):
        for k in range(1, 7):
            d1[place[y], place[(y + k) % 48]] += FIRST[k - 1]
            d1[place[y], place[(y - k) % 48]] -= FIRST[k - 1]
            d2[place[y], place[(y + k) % 48]] += SECOND[k]
            d2[place[y], place[(y - k) % 48]] += SECOND[k]
    a1, a2 = two_parts(np.concatenate([(G01 / G02) * d1, SIGMA * d2]))
    b1, b2 = two_parts(SIGMA * 2.0 * G12 * d1)
    return np.concatenate([a1, a1, a2], axis=1), np.concatenate([b1, b1, b2], axis=1)


def split(value):
    hi = value.astype(BF16)
    lo = (value - hi.astype(F32)).astype(BF16)
    return hi, lo


def kernel(
    orb_hbm,
    pot_hbm,
    mz_hbm,
    my1_hbm,
    my2_hbm,
    out_hbm,
    orb,
    pot,
    mz,
    my1,
    my2,
    out,
    sm,
    sr,
    sz,
    spm,
    spr,
    v,
    rr,
    vp,
    vq,
    rp,
    zd,
    zs,
    zr,
    cs,
    cr,
    part,
    wf,
    v1,
    v2,
    h1,
    h2,
    tz,
    yf,
    ro,
    om,
    orr,
    load_s,
    tin_s,
    tin_r,
    zd_s,
    zd_r,
    zx_s,
    zx_r,
    xc_s,
    xc_r,
    to_s,
    to_r,
):
    gx = lax.axis_index("gx")
    gy = lax.axis_index("gy")
    gz = lax.axis_index("gz")
    half = gy // 2
    core = lax.rem(gy, 2)
    far = 1 - half
    near = [far * 2 + core, far * 2 + 1 - core, half * 2 + 1 - core]
    x_at = [{"gx": lax.rem(gx + 3, 4)}, {"gx": lax.rem(gx + 1, 4)}]
    z_to = [lax.rem(gz + 7, 8), lax.rem(gz + 1, 8)]
    z_at = [{"gz": z_to[0]}, {"gz": z_to[1]}]
    z_near = [gy] + near

    def copy(src, dst, send, recv, device):
        return pltpu.make_async_remote_copy(
            src_ref=src, dst_ref=dst, send_sem=send, recv_sem=recv, device_id=device, device_id_type=MESH
        )

    barrier = pltpu.get_barrier_semaphore()
    friends = x_at + [{"gy": n} for n in near]
    friends += [{"gy": n, "gz": z} for n in z_near for z in z_to]
    for device in friends:
        pl.semaphore_signal(barrier, inc=1, device_id=device, device_id_type=MESH)

    loads = [
        pltpu.make_async_copy(orb_hbm.at[:, 0], orb.at[0], load_s.at[0]),
        pltpu.make_async_copy(orb_hbm.at[:, 1], orb.at[1], load_s.at[1]),
        pltpu.make_async_copy(pot_hbm, pot, load_s.at[2]),
        pltpu.make_async_copy(mz_hbm, mz, load_s.at[3]),
        pltpu.make_async_copy(my1_hbm, my1, load_s.at[4]),
        pltpu.make_async_copy(my2_hbm, my2, load_s.at[5]),
    ]
    for one in loads:
        one.start()

    low_half = lax.broadcasted_iota(jnp.int32, (8, 128), 0) < 4
    lane8 = lax.broadcasted_iota(jnp.int32, (8, 128), 1)
    even_lane = lax.rem(lane8, 12) < 6
    lane = lax.broadcasted_iota(jnp.int32, (48, 128), 1)

    def turn(a):
        return pltpu.roll(a, 4, 0)

    def pair(a, b):
        return jnp.where(low_half, a, turn(b)), jnp.where(low_half, turn(a), b)

    def lanes(a, by):
        return a if by % 128 == 0 else pltpu.roll(a, by % 128, 1)

    orb_rows = orb.reshape(2304, 128)
    out_rows = out.reshape(2304, 128)
    started = []

    def start(c):
        c.start()
        started.append(c)

    def tin(c, rel):
        to = {"gy": near[rel]}
        return [
            copy(sm.at[c, near[rel]], v.at[c, 0, :, gy], tin_s.at[c, rel, 0], tin_r.at[c, rel, 0], to),
            copy(sr.at[c, near[rel]], rr.at[c, gy], tin_s.at[c, rel, 1], tin_r.at[c, rel, 1], to),
        ]

    def vin(rel):
        to = {"gy": near[rel]}
        return [
            copy(spm, vp.at[:, gy], tin_s.at[4, rel, 0], tin_r.at[4, rel, 0], to),
            copy(spr, rp.at[gy], tin_s.at[4, rel, 1], tin_r.at[4, rel, 1], to),
        ]

    def vpass():
        to = {"gy": near[2]}
        return [
            copy(vp.at[:, near[0]], vp.at[:, near[0]], tin_s.at[4, 1, 0], tin_r.at[4, 1, 0], to),
            copy(rp.at[near[0]], rp.at[near[0]], tin_s.at[4, 1, 1], tin_r.at[4, 1, 1], to),
        ]

    def zin(c, k, side):
        return copy(
            sz.at[c, z_near[k], side],
            zd.at[c, 1 - side, gy],
            zd_s.at[c, k, side],
            zd_r.at[c, k, side],
            {"gy": z_near[k], "gz": z_to[side]},
        )

    def prepare_potential():
        for x in range(12):
            spm[x] = pot[x, 0:8]
        for p in range(6):
            spr[p] = jnp.concatenate([pot[2 * p, 8:12], pot[2 * p + 1, 8:12]], axis=0)
        vp[:, gy] = spm[...]
        rp[gy] = spr[...]

    def prepare(c):
        def band(g, carry):
            b = 4 * (c % 2) + g
            main = [None] * 2
            rest = [None] * 4
            for x in range(12):
                val = orb_rows[pl.ds(1152 * (c // 2) + x * ROWS + b, 8, stride=STRIDE), :]
                sm[c, g, x] = val
                for side in range(2):
                    r = lanes(val, 6 * x + 6 * side)
                    main[side] = r if x == 0 else jnp.where(lane8 >= 6 * x, r, main[side])
            for p in range(6):
                lo = orb_rows[pl.ds(1152 * (c // 2) + 2 * p * ROWS + 8 * STRIDE + b, 4, stride=STRIDE), :]
                hi = orb_rows[pl.ds(1152 * (c // 2) + (2 * p + 1) * ROWS + 8 * STRIDE + b, 4, stride=STRIDE), :]
                val = jnp.concatenate([lo, hi], axis=0)
                sr[c, g, p] = val
                for side in range(2):
                    for odd in range(2):
                        r = lanes(val, 12 * p + 6 * odd + 6 * side)
                        at = 2 * side + odd
                        rest[at] = r if p == 0 else jnp.where(lane8 >= 12 * p + 6 * odd, r, rest[at])
            for side in range(2):
                sz[c, g, side, 0] = main[side]
                sz[c, g, side, 1] = jnp.where(low_half, rest[2 * side], rest[2 * side + 1])
            return carry

        lax.fori_loop(0, 4, band, 0)

    def send_in(c):
        for k in (1, 2, 0, 3):
            for side in range(2):
                start(zin(c, k, side))
        for rel in range(3):
            for one in tin(c, rel):
                start(one)
        v[c, 0, :, gy] = sm[c, gy]
        rr[c, gy] = sr[c, gy]

    def assemble(rest, dest):
        for p in range(6):
            for t in range(2):
                even, odd = pair(rest[2 * t, p], rest[2 * t + 1, p])
                dest(2 * p, 4 + t, even)
                dest(2 * p + 1, 4 + t, odd)

    def zx(c, side):
        return copy(zs.at[c, side], zr.at[c, 1 - side], zx_s.at[c, side], zx_r.at[c, side], z_at[side])

    def edges(c):
        low = None
        high = None
        for x in range(12):
            val = v[c, 1, x].reshape(48, 128)
            a = lanes(val, 6 * x)
            b = lanes(val, 6 * x + 6)
            low = a if x == 0 else jnp.where(lane >= 6 * x, a, low)
            high = b if x == 0 else jnp.where(lane >= 6 * x, b, high)
        zs[c, 0] = low.reshape(6, 8, 128)
        zs[c, 1] = high.reshape(6, 8, 128)
        for side in range(2):
            start(zx(c, side))

    def stage_a(c):
        for rel in range(3):
            for one in tin(c, rel):
                one.wait_recv()

        def dest(x, t, value):
            v[c, 0, x, t] = value

        assemble(rr.at[c], dest)

    def xc(c, step, side, piece):
        return copy(
            cs.at[c, step, side, piece],
            cr.at[c, step, side, piece],
            xc_s.at[c, step, side, piece],
            xc_r.at[c, step, side, piece],
            x_at[side],
        )

    def halo(c, step, side):
        if step == 1:
            zx(c, 1 - side).wait_recv()
            return zr[c, side].reshape(48, 128)
        for k in range(4):
            zin(c, k, 1 - side).wait_recv()
        tiles = [zd[c, side, s, 0] for s in range(4)]
        for t in range(2):
            a = zd[c, side, 2 * t, 1]
            b = zd[c, side, 2 * t + 1, 1]
            a = jnp.where(even_lane, a, turn(a))
            b = jnp.where(even_lane, turn(b), b)
            tiles.append(jnp.where(low_half, a, b))
        return jnp.concatenate(tiles, axis=0)

    def piece_tile(piece, i):
        block = far if piece == 0 else half
        return 2 * block + i if i < 2 else 4 + block

    def stage_b(c, step):
        for x in range(12):
            a, b = split(v[c, step, x].reshape(48, 128))
            v1[x] = a
            v2[x] = b
        below = halo(c, step, 0)
        above = halo(c, step, 1)
        for x in range(12):
            up = lanes(above, 128 - 6 * x)
            down = lanes(below, 122 - 6 * x)
            h = jnp.where(lane < 6, up, jnp.where(lane >= 122, down, 0.0))
            a, b = split(h)
            h1[x] = a
            h2[x] = b
        f1 = v1[...].reshape(576, 128)
        f2 = v2[...].reshape(576, 128)
        g1 = h1[...].reshape(576, 128)
        g2 = h2[...].reshape(576, 128)
        acc = jnp.dot(jnp.concatenate([f1, f2], axis=1), mz[0], preferred_element_type=F32)
        acc += jnp.dot(jnp.concatenate([f1, g1], axis=1), mz[1], preferred_element_type=F32)
        acc += jnp.dot(jnp.concatenate([g1, g2], axis=1), mz[2], preferred_element_type=F32)
        tz[...] = acc
        for xp in range(6):
            x0, x1 = 2 * xp, 2 * xp + 1
            a = jnp.concatenate([v1[x0], v1[x1]], axis=1)
            b = jnp.concatenate([v2[x0], v2[x1]], axis=1)
            q = jnp.dot(my1[...], jnp.concatenate([a, b, a], axis=0), preferred_element_type=F32)
            t = jnp.concatenate([tz[48 * x0 : 48 * x0 + 48, 0:128], tz[48 * x1 : 48 * x1 + 48, 0:128]], axis=1)
            s = jnp.concatenate([tz[48 * x0 : 48 * x0 + 48, 128:256], tz[48 * x1 : 48 * x1 + 48, 128:256]], axis=1)
            ta, tb = split(t)
            r = jnp.dot(my2[...], jnp.concatenate([ta, tb, ta], axis=0), preferred_element_type=F32)
            w = q[0:48] + t
            r = r + q[48:96] + s
            for i, x in enumerate((x0, x1)):
                wf[x] = w[:, 128 * i : 128 * i + 128].reshape(6, 8, 128)
                part[c, x] = r[:, 128 * i : 128 * i + 128].reshape(6, 8, 128)

        for piece in range(2):
            block = far if piece == 0 else half

            def tile(i, carry):
                t = (i // 2) * (4 + block) + (1 - i // 2) * (2 * block + i)
                acc = [None] * 24
                for j in range(12):
                    vj = v[c, step, j, t]
                    wj = wf[j, t]
                    for k in range(1, 7):
                        cv = XC[k] * vj
                        aw = XA[k - 1] * wj
                        lo, hi = j + 6 - k, j + 6 + k
                        acc[lo] = cv + aw if acc[lo] is None else acc[lo] + (cv + aw)
                        acc[hi] = cv - aw if acc[hi] is None else acc[hi] + (cv - aw)
                for j in range(6):
                    cs[c, step, 0, piece, j, i] = acc[j]
                    cs[c, step, 1, piece, j, i] = acc[18 + j]
                for j in range(12):
                    part[c, j, t] = part[c, j, t] + acc[6 + j]
                return carry

            lax.fori_loop(0, 3, tile, 0)
            for side in range(2):
                start(xc(c, step, side, piece))

    def to(c, rel):
        at = {"gy": near[rel]}
        return [
            copy(yf.at[c, :, near[rel]], om.at[c, gy], to_s.at[c, rel, 0], to_r.at[c, rel, 0], at),
            copy(ro.at[c, near[rel]], orr.at[c, gy], to_s.at[c, rel, 1], to_r.at[c, rel, 1], at),
        ]

    def stage_c(c, step):
        for piece in range(2):
            for side in range(2):
                xc(c, step, side, piece).wait_recv()
            for i in range(3):
                t = piece_tile(piece, i)
                got = jnp.concatenate([cr[c, step, 1, piece, :, i], cr[c, step, 0, piece, :, i]], axis=0)
                y = part[c, :, t] + got + vq[:, t] * v[c, step, :, t]
                if step == 0:
                    v[c, 1, :, t] = y
                else:
                    yf[c, :, t] = 2.0 * y - v[c, 0, :, t]
            if step == 0:
                continue
            block = far if piece == 0 else half
            for p in range(6):
                even, odd = pair(yf[c, 2 * p, 4 + block], yf[c, 2 * p + 1, 4 + block])
                ro[c, 2 * block, p] = even
                ro[c, 2 * block + 1, p] = odd
            for rel in (0, 1) if piece == 0 else (2,):
                for one in to(c, rel):
                    start(one)
        if step == 0:
            edges(c)
            return
        om[c, gy] = yf[c, :, gy]
        orr[c, gy] = ro[c, gy]

    def stage_d(c):
        for rel in (2, 0, 1):
            for one in to(c, rel):
                one.wait_recv()

        def band(g, carry):
            b = 4 * (c % 2) + g
            for x in range(12):
                out_rows[pl.ds(1152 * (c // 2) + x * ROWS + b, 8, stride=STRIDE), :] = om[c, g, x]
            for p in range(6):
                r = orr[c, g, p]
                out_rows[pl.ds(1152 * (c // 2) + 2 * p * ROWS + 8 * STRIDE + b, 4, stride=STRIDE), :] = r[0:4]
                out_rows[pl.ds(1152 * (c // 2) + (2 * p + 1) * ROWS + 8 * STRIDE + b, 4, stride=STRIDE), :] = r[4:8]
            return carry

        lax.fori_loop(0, 4, band, 0)

    def store(h):
        return pltpu.make_async_copy(out.at[h], out_hbm.at[:, h], load_s.at[6 + h])

    loads[0].wait()
    prepare(0)
    pl.semaphore_wait(barrier, len(friends))
    send_in(0)
    prepare(1)
    send_in(1)
    loads[2].wait()
    prepare_potential()
    for rel in (0, 2):
        for one in vin(rel):
            start(one)
    loads[1].wait()
    for c in (2, 3):
        prepare(c)
        send_in(c)
    for one in loads[3:]:
        one.wait()

    stage_a(0)
    stage_b(0, 0)
    stage_a(1)
    stage_b(1, 0)
    for one in vin(0):
        one.wait_recv()
    for one in vpass():
        start(one)
    for one in vin(2) + vpass():
        one.wait_recv()

    def scaled(a):
        return (a - CENTER) * (1.0 / HALF_WIDTH) + 3.0 * XC[0]

    def place(x, t, value):
        vq[x, t] = scaled(value)

    assemble(rp, place)
    for x in range(12):
        vq[x, 0:4] = scaled(vp[x])
    stage_c(0, 0)
    stage_a(2)
    stage_b(2, 0)
    stage_c(1, 0)
    stage_a(3)
    stage_b(3, 0)
    stage_b(0, 1)
    stage_c(2, 0)
    stage_b(1, 1)
    stage_c(3, 0)
    stage_b(2, 1)
    stage_c(0, 1)
    stage_b(3, 1)
    stage_c(1, 1)
    stage_c(2, 1)
    stage_d(0)
    stage_c(3, 1)
    stage_d(1)
    store(0).start()
    stage_d(2)
    stage_d(3)
    store(1).start()
    store(0).wait()
    store(1).wait()
    for one in started:
        one.wait_send()


def local(orbitals, potential):
    rows = jnp.transpose(orbitals, (1, 2, 0, 3)).reshape(144, 2, 8, 128)
    my1, my2 = y_matrices()
    anywhere = pl.BlockSpec(memory_space=pl.ANY)
    tile = (6, 8, 128)
    slab = (12, *tile)
    sem = pltpu.SemaphoreType.DMA

    def vmem(*shape, dtype=F32):
        return pltpu.VMEM(shape, dtype)

    out = pl.pallas_call(
        kernel,
        out_shape=jax.ShapeDtypeStruct((144, 2, 8, 128), F32),
        in_specs=[anywhere] * 5,
        out_specs=anywhere,
        scratch_shapes=[
            vmem(2, 144, 8, 128),
            vmem(12, 12, 128),
            vmem(3, 256, 256, dtype=BF16),
            vmem(96, 144, dtype=BF16),
            vmem(48, 144, dtype=BF16),
            vmem(2, 144, 8, 128),
            vmem(4, 4, 12, 8, 128),
            vmem(4, 4, *tile),
            vmem(4, 4, 2, 2, 8, 128),
            vmem(12, 8, 128),
            vmem(*tile),
            vmem(4, 2, *slab),
            vmem(4, 4, *tile),
            vmem(12, 4, 8, 128),
            vmem(*slab),
            vmem(4, *tile),
            vmem(4, 2, 4, 2, 8, 128),
            vmem(4, 2, *tile),
            vmem(4, 2, *tile),
            vmem(4, 2, 2, 2, 6, 3, 8, 128),
            vmem(4, 2, 2, 2, 6, 3, 8, 128),
            vmem(4, *slab),
            vmem(*slab),
            vmem(12, 48, 128, dtype=BF16),
            vmem(12, 48, 128, dtype=BF16),
            vmem(12, 48, 128, dtype=BF16),
            vmem(12, 48, 128, dtype=BF16),
            vmem(576, 256),
            vmem(4, *slab),
            vmem(4, 4, *tile),
            vmem(4, 4, 12, 8, 128),
            vmem(4, 4, *tile),
            sem((8,)),
            sem((5, 3, 2)),
            sem((5, 3, 2)),
            sem((4, 4, 2)),
            sem((4, 4, 2)),
            sem((4, 2)),
            sem((4, 2)),
            sem((4, 2, 2, 2)),
            sem((4, 2, 2, 2)),
            sem((4, 3, 2)),
            sem((4, 3, 2)),
        ],
        compiler_params=pltpu.CompilerParams(
            collective_id=0, has_side_effects=True, vmem_limit_bytes=60 * 1024 * 1024
        ),
    )(rows, potential, jnp.asarray(z_matrices()), jnp.asarray(my1), jnp.asarray(my2))
    return jnp.transpose(out.reshape(12, 12, 16, 128), (2, 0, 1, 3))


def solution(mesh):
    return jax.shard_map(
        local,
        mesh=mesh,
        in_specs=(P(None, "gx", "gy", "gz"), P("gx", "gy", "gz")),
        out_specs=P(None, "gx", "gy", "gz"),
        check_vma=False,
    )
```

time: 62.7 us -> 56.1 us (0.89)
  Pallas kernels: 60.2 us -> 53.6 us
    pallas_call x1, Pallas kernels: 60.2 us -> 53.6 us  [local(): pl.pallas_call(kernel, out_shape=jax.ShapeDtypeStruct((144, 2, 8, 128), F...]
where the time goes in v2:
time: 56.1 us; the launch traced here: 55.9 us
  Pallas kernels  53.6 us (96%)
  local copies, waits for them, and re-layouts  2.36 us (4%)
    pallas_call x1, Pallas kernels, local(): pl.pallas_call(kernel, out_shape=jax.ShapeDtypeStruct((144, 2, 8, 128), F...  53.6 us
    unnamed x1, local copies, waits for them, and re-layouts  2.36 us

profile of v2, /device:TPU:1, one launch (start us, length us, event | category | flops | bytes accessed | tf_op | source)
XLA Modules:
  0.0 55.9 jit_solution(10579201546356434690)
XLA Ops:
  0.0 53.6 %shard_map.55 = f32[144,2,8,128]{3,2,1,0:T(8,128)} custom-call(f32[144,2,8,128]{3,2,1,0:T(8,128)} %bitcast.7, f32[12,12,128]{2,1,0:T(8,128)} %pot_hbm.1, bf16[3,256,256]{2,1,0:T(8,128)(2,1)} %constant.6.clone.mz_hbm, bf16[96,144]{1,0:T(8,128)(2,1)} %constant.7.clone.my1_hbm, bf16[48,144]{1,0:T(8,128)(2,1)} %constant.8.clone.my2_hbm), custom_call_target="tpu_custom_call" | custom-call | tf_op jit(solution)/shard_map/pallas_call | solution.py:530
  53.6 2.4 %copy.7 = f32[16,12,12,128]{3,0,2,1:T(8,128)} copy(f32[16,12,12,128]{3,0,2,1:T(8,128)} %bitcast.6) | data formatting | bytes 2359296

commit v3 on v2

v3 whole, which is shorter than its diff:
```python
import functools

import jax
import jax.numpy as jnp
import numpy as np
from jax import lax
from jax.experimental import pallas as pl
from jax.experimental.pallas import tpu as pltpu
from jax.sharding import PartitionSpec as P

MESH = pl.DeviceIdType.MESH
SECOND = (
    -5369.0 / 1800.0,
    12.0 / 7.0,
    -15.0 / 56.0,
    10.0 / 189.0,
    -1.0 / 112.0,
    2.0 / 1925.0,
    -1.0 / 16632.0,
)
FIRST = (6.0 / 7.0, -15.0 / 56.0, 5.0 / 63.0, -1.0 / 56.0, 3.0 / 385.0, -1.0 / 792.0)
G01, G02, G12 = 0.25, 0.15, 0.2
CENTER = 10.5
HALF_WIDTH = 9.5
SIGMA = -0.5 / HALF_WIDTH

XC = [SIGMA * c for c in SECOND]
XA = [[SIGMA * 2.0 * g * a for a in FIRST] for g in (G02, G12)]

F32 = jnp.float32
BF16 = jnp.bfloat16


def order_of_rows():
    rows = []
    for s in range(4):
        rows += [12 * s + r for r in range(8)]
    for s in range(4):
        rows += [12 * s + 8 + r for r in range(4)]
    return rows


def two_parts(m):
    hi = m.astype(np.float32).astype(jnp.bfloat16)
    lo = (m - hi.astype(np.float64)).astype(np.float32).astype(jnp.bfloat16)
    return hi, lo


def z_matrices():
    m = np.zeros((140, 256))
    for z in range(128):
        for k in range(1, 7):
            m[z + 6 + k, z] += FIRST[k - 1]
            m[z + 6 - k, z] -= FIRST[k - 1]
            m[z + 6 + k, 128 + z] += SIGMA * SECOND[k]
            m[z + 6 - k, 128 + z] += SIGMA * SECOND[k]
    inside = m[6:134]
    halo = np.zeros((128, 256))
    halo[122:128] = m[0:6]
    halo[0:6] = m[134:140]
    i1, i2 = two_parts(inside)
    h1, h2 = two_parts(halo)
    return np.stack([np.concatenate([i1, i1]), np.concatenate([i2, h1]), np.concatenate([h2, h1])])


def y_matrices(g_here, g_other):
    rows = order_of_rows()
    place = {y: r for r, y in enumerate(rows)}
    d1 = np.zeros((48, 48))
    d2 = np.zeros((48, 48))
    for y in range(48):
        for k in range(1, 7):
            d1[place[y], place[(y + k) % 48]] += FIRST[k - 1]
            d1[place[y], place[(y - k) % 48]] -= FIRST[k - 1]
            d2[place[y], place[(y + k) % 48]] += SECOND[k]
            d2[place[y], place[(y - k) % 48]] += SECOND[k]
    a1, a2 = two_parts(np.concatenate([(G01 / g_here) * d1, SIGMA * d2]))
    b1, b2 = two_parts(SIGMA * 2.0 * g_other * d1)
    return np.concatenate([a1, a1, a2], axis=1), np.concatenate([b1, b1, b2], axis=1)


def split(value):
    hi = value.astype(BF16)
    lo = (value - hi.astype(F32)).astype(BF16)
    return hi, lo


def picked(c, g, i, rest):
    if c < 2:
        first, step = i * 96, 8
    else:
        first, step = 1152 + i * 8, 96
    first = first + 4 * (c % 2) + g
    return pl.ds(first + 8 * step, 4, stride=step) if rest else pl.ds(first, 8, stride=step)


def kernel(
    orb_hbm,
    pot_hbm,
    mz_hbm,
    my1_hbm,
    my2_hbm,
    om,
    orr,
    orb,
    pot,
    mz,
    my1,
    my2,
    sm,
    sr,
    sz,
    spm,
    spr,
    v,
    rr,
    vp,
    vq,
    rp,
    zd,
    zs,
    zr,
    cs,
    cr,
    part,
    wf,
    v1,
    v2,
    h1,
    h2,
    tz,
    yf,
    ro,
    load_s,
    sent,
    tin_r,
    vin_r,
    zd_r,
    zx_r,
    xc_r,
    to_r,
):
    gx = lax.axis_index("gx")
    gy = lax.axis_index("gy")
    gz = lax.axis_index("gz")
    axis = ("gy", "gx")
    pos = (gy, gx)
    half = [p // 2 for p in pos]
    core = [lax.rem(p, 2) for p in pos]
    far = [1 - h for h in half]
    near = [[f * 2 + k, f * 2 + 1 - k, h * 2 + 1 - k] for f, h, k in zip(far, half, core)]
    side_at = (
        ({"gx": lax.rem(gx + 3, 4)}, {"gx": lax.rem(gx + 1, 4)}),
        ({"gy": lax.rem(gy + 3, 4)}, {"gy": lax.rem(gy + 1, 4)}),
    )
    z_to = [lax.rem(gz + 7, 8), lax.rem(gz + 1, 8)]
    z_at = [{"gz": z_to[0]}, {"gz": z_to[1]}]
    z_near = [[pos[r]] + near[r] for r in range(2)]

    def copy(src, dst, send, recv, device):
        return pltpu.make_async_remote_copy(
            src_ref=src, dst_ref=dst, send_sem=send, recv_sem=recv, device_id=device, device_id_type=MESH
        )

    barrier = pltpu.get_barrier_semaphore()
    friends = [{axis[r]: n} for r in range(2) for n in near[r]]
    friends += z_at
    friends += [{axis[r]: n, "gz": z} for r in range(2) for n in near[r] for z in z_to]
    for device in friends:
        pl.semaphore_signal(barrier, inc=1, device_id=device, device_id_type=MESH)

    loads = [
        pltpu.make_async_copy(orb_hbm.at[:, 0], orb.at[0], load_s.at[0]),
        pltpu.make_async_copy(orb_hbm.at[:, 1], orb.at[1], load_s.at[1]),
        pltpu.make_async_copy(pot_hbm, pot, load_s.at[2]),
        pltpu.make_async_copy(mz_hbm, mz, load_s.at[3]),
        pltpu.make_async_copy(my1_hbm, my1, load_s.at[4]),
        pltpu.make_async_copy(my2_hbm, my2, load_s.at[5]),
    ]
    for one in loads:
        one.start()

    low_half = lax.broadcasted_iota(jnp.int32, (8, 128), 0) < 4
    lane8 = lax.broadcasted_iota(jnp.int32, (8, 128), 1)
    even_lane = lax.rem(lane8, 12) < 6
    lane = lax.broadcasted_iota(jnp.int32, (48, 128), 1)

    def turn(a):
        return pltpu.roll(a, 4, 0)

    def pair(a, b):
        return jnp.where(low_half, a, turn(b)), jnp.where(low_half, turn(a), b)

    def lanes(a, by):
        return a if by % 128 == 0 else pltpu.roll(a, by % 128, 1)

    orb_rows = orb.reshape(2304, 128)
    def start(c):
        c.start()

    def arrived(ref, sem):
        copy(ref, ref, sem, sem, {"gx": gx}).wait_recv()

    def tin(c, rel):
        r = c // 2
        peer = near[r][rel]
        to = {axis[r]: peer}
        return [
            copy(sm.at[c, peer], v.at[c, 0, :, pos[r]], sent.at[0], tin_r.at[c, 0], to),
            copy(sr.at[c, peer], rr.at[c, pos[r]], sent.at[1], tin_r.at[c, 1], to),
        ]

    def vin(r, rel):
        to = {axis[r]: near[r][rel]}
        return [
            copy(spm.at[r], vp.at[r, :, pos[r]], sent.at[2], vin_r.at[r, rel, 0], to),
            copy(spr.at[r], rp.at[r, pos[r]], sent.at[3], vin_r.at[r, rel, 1], to),
        ]

    def vpass(r):
        if r == 0:
            other, to = near[0][0], {"gy": near[0][2]}
            return [
                copy(vp.at[0, :, other], vp.at[0, :, other], sent.at[2], vin_r.at[0, 1, 0], to),
                copy(rp.at[0, other], rp.at[0, other], sent.at[3], vin_r.at[0, 1, 1], to),
            ]
        copies = []
        for k, (source, target) in enumerate(((1, 2), (2, 1))):
            other, to = near[1][source], {"gx": near[1][target]}
            lead, rest = vp.at[1, 6 * k : 6 * k + 6, other], rp.at[1, other, 3 * k : 3 * k + 3]
            copies.append(copy(lead, lead, sent.at[2], vin_r.at[1, 0, 0], to))
            copies.append(copy(rest, rest, sent.at[3], vin_r.at[1, 0, 1], to))
        return copies

    def zin(c, k, side):
        r = c // 2
        return copy(
            sz.at[c, z_near[r][k], side],
            zd.at[c, 1 - side, pos[r]],
            sent.at[4],
            zd_r.at[c],
            {axis[r]: z_near[r][k], "gz": z_to[side]},
        )

    def prepare_potential(r):
        def rows(i, start, count):
            if r == 0:
                return pot[i, start : start + count]
            return jnp.concatenate([pot[start + k, i : i + 1] for k in range(count)], axis=0)

        for i in range(12):
            spm[r, i] = rows(i, 0, 8)
        for p in range(6):
            spr[r, p] = jnp.concatenate([rows(2 * p, 8, 4), rows(2 * p + 1, 8, 4)], axis=0)
        vp[r, :, pos[r]] = spm[r]
        rp[r, pos[r]] = spr[r]

    def send_potential(r):
        for rel in (r, 2):
            for one in vin(r, rel):
                start(one)

    def pass_potential(r):
        for rel in (r, 2):
            for one in vin(r, rel):
                one.wait_recv()
        for one in vpass(r):
            start(one)

    def finish_potential(r):
        arrived(vp.at[r, :, 0], vin_r.at[r, 1 - r, 0])
        arrived(rp.at[r, 0], vin_r.at[r, 1 - r, 1])

        def scaled(a):
            return (a - CENTER) * (1.0 / HALF_WIDTH) + 3.0 * XC[0]

        def place(x, t, value):
            vq[r, x, t] = scaled(value)

        assemble(rp.at[r], place)
        for x in range(12):
            vq[r, x, 0:4] = scaled(vp[r, x])

    def prepare(c):
        def band(g, carry):
            main = [None] * 2
            rest = [None] * 4
            for x in range(12):
                val = orb_rows[picked(c, g, x, False), :]
                sm[c, g, x] = val
                for side in range(2):
                    r = lanes(val, 6 * x + 6 * side)
                    main[side] = r if x == 0 else jnp.where(lane8 >= 6 * x, r, main[side])
            for p in range(6):
                lo = orb_rows[picked(c, g, 2 * p, True), :]
                hi = orb_rows[picked(c, g, 2 * p + 1, True), :]
                val = jnp.concatenate([lo, hi], axis=0)
                sr[c, g, p] = val
                for side in range(2):
                    for odd in range(2):
                        r = lanes(val, 12 * p + 6 * odd + 6 * side)
                        at = 2 * side + odd
                        rest[at] = r if p == 0 else jnp.where(lane8 >= 12 * p + 6 * odd, r, rest[at])
            for side in range(2):
                sz[c, g, side, 0] = main[side]
                sz[c, g, side, 1] = jnp.where(low_half, rest[2 * side], rest[2 * side + 1])
            return carry

        lax.fori_loop(0, 4, band, 0)

    def send_in(c):
        for k in (1, 2, 0, 3):
            for side in range(2):
                start(zin(c, k, side))
        for rel in range(3):
            for one in tin(c, rel):
                start(one)
        me = pos[c // 2]
        v[c, 0, :, me] = sm[c, me]
        rr[c, me] = sr[c, me]

    def assemble(rest, dest):
        for p in range(6):
            for t in range(2):
                even, odd = pair(rest[2 * t, p], rest[2 * t + 1, p])
                dest(2 * p, 4 + t, even)
                dest(2 * p + 1, 4 + t, odd)

    def zx(c, side):
        return copy(zs.at[c, side], zr.at[c, 1 - side], sent.at[5], zx_r.at[c, side], z_at[side])

    def edges(c):
        low = None
        high = None
        for x in range(12):
            val = v[c, 1, x].reshape(48, 128)
            a = lanes(val, 6 * x)
            b = lanes(val, 6 * x + 6)
            low = a if x == 0 else jnp.where(lane >= 6 * x, a, low)
            high = b if x == 0 else jnp.where(lane >= 6 * x, b, high)
        zs[c, 0] = low.reshape(6, 8, 128)
        zs[c, 1] = high.reshape(6, 8, 128)
        for side in range(2):
            start(zx(c, side))

    def stage_a(c):
        arrived(v.at[c, 0, :, 0:3], tin_r.at[c, 0])
        arrived(rr.at[c, 0:3], tin_r.at[c, 1])

        def dest(x, t, value):
            v[c, 0, x, t] = value

        assemble(rr.at[c], dest)

    def xc(c, step, side, piece):
        return copy(
            cs.at[c, step, piece, side],
            cr.at[c, step, piece, side],
            sent.at[6],
            xc_r.at[c, step, piece],
            side_at[c // 2][side],
        )

    def halo(c, step, side):
        if step == 1:
            zx(c, 1 - side).wait_recv()
            return zr[c, side].reshape(48, 128)
        if side == 0:
            arrived(zd.at[c], zd_r.at[c])
        tiles = [zd[c, side, s, 0] for s in range(4)]
        for t in range(2):
            a = zd[c, side, 2 * t, 1]
            b = zd[c, side, 2 * t + 1, 1]
            a = jnp.where(even_lane, a, turn(a))
            b = jnp.where(even_lane, turn(b), b)
            tiles.append(jnp.where(low_half, a, b))
        return jnp.concatenate(tiles, axis=0)

    def block_of(c, piece):
        return far[c // 2] if piece == 0 else half[c // 2]

    def piece_tile(c, piece, i):
        block = block_of(c, piece)
        return 2 * block + i if i < 2 else 4 + block

    def stage_b(c, step, between=()):
        for x in range(12):
            a, b = split(v[c, step, x].reshape(48, 128))
            v1[x] = a
            v2[x] = b
        below = halo(c, step, 0)
        above = halo(c, step, 1)
        for x in range(12):
            up = lanes(above, 128 - 6 * x)
            down = lanes(below, 122 - 6 * x)
            h = jnp.where(lane < 6, up, jnp.where(lane >= 122, down, 0.0))
            a, b = split(h)
            h1[x] = a
            h2[x] = b
        for part_rows in range(2):
            xs = slice(6 * part_rows, 6 * part_rows + 6)
            f1 = v1[xs].reshape(288, 128)
            f2 = v2[xs].reshape(288, 128)
            g1 = h1[xs].reshape(288, 128)
            g2 = h2[xs].reshape(288, 128)
            acc = jnp.dot(jnp.concatenate([f1, f2], axis=1), mz[0], preferred_element_type=F32)
            acc += jnp.dot(jnp.concatenate([f1, g1], axis=1), mz[1], preferred_element_type=F32)
            acc += jnp.dot(jnp.concatenate([g1, g2], axis=1), mz[2], preferred_element_type=F32)
            tz[288 * part_rows : 288 * part_rows + 288] = acc
        for xp in range(6):
            x0, x1 = 2 * xp, 2 * xp + 1
            a = jnp.concatenate([v1[x0], v1[x1]], axis=1)
            b = jnp.concatenate([v2[x0], v2[x1]], axis=1)
            q = jnp.dot(my1[c // 2], jnp.concatenate([a, b, a], axis=0), preferred_element_type=F32)
            t = jnp.concatenate([tz[48 * x0 : 48 * x0 + 48, 0:128], tz[48 * x1 : 48 * x1 + 48, 0:128]], axis=1)
            s = jnp.concatenate([tz[48 * x0 : 48 * x0 + 48, 128:256], tz[48 * x1 : 48 * x1 + 48, 128:256]], axis=1)
            ta, tb = split(t)
            r = jnp.dot(my2[c // 2], jnp.concatenate([ta, tb, ta], axis=0), preferred_element_type=F32)
            w = q[0:48] + t
            r = r + q[48:96] + s
            for i, x in enumerate((x0, x1)):
                wf[x] = w[:, 128 * i : 128 * i + 128].reshape(6, 8, 128)
                part[c, x] = r[:, 128 * i : 128 * i + 128].reshape(6, 8, 128)

        for r in between:
            pass_potential(r)
        for piece in range(2):
            block = block_of(c, piece)

            def tile(i, carry):
                t = (i // 2) * (4 + block) + (1 - i // 2) * (2 * block + i)
                acc = [None] * 24
                for j in range(12):
                    vj = v[c, step, j, t]
                    wj = wf[j, t]
                    for k in range(1, 7):
                        cv = XC[k] * vj
                        aw = XA[c // 2][k - 1] * wj
                        lo, hi = j + 6 - k, j + 6 + k
                        acc[lo] = cv + aw if acc[lo] is None else acc[lo] + (cv + aw)
                        acc[hi] = cv - aw if acc[hi] is None else acc[hi] + (cv - aw)
                for j in range(6):
                    cs[c, step, piece, 0, j, i] = acc[j]
                    cs[c, step, piece, 1, j, i] = acc[18 + j]
                for j in range(12):
                    part[c, j, t] = part[c, j, t] + acc[6 + j]
                return carry

            lax.fori_loop(0, 3, tile, 0)
            for side in range(2):
                start(xc(c, step, side, piece))

    def to(c, rel):
        r = c // 2
        peer = near[r][rel]
        at = {axis[r]: peer}
        return [
            copy(yf.at[c, :, peer], om.at[c, pos[r]], sent.at[7], to_r.at[c, 0], at),
            copy(ro.at[c, peer], orr.at[c, pos[r]], sent.at[8], to_r.at[c, 1], at),
        ]

    def stage_c(c, step):
        for piece in range(2):
            arrived(cr.at[c, step, piece], xc_r.at[c, step, piece])
            for i in range(3):
                t = piece_tile(c, piece, i)
                got = jnp.concatenate([cr[c, step, piece, 1, :, i], cr[c, step, piece, 0, :, i]], axis=0)
                y = part[c, :, t] + got + vq[c // 2, :, t] * v[c, step, :, t]
                if step == 0:
                    v[c, 1, :, t] = y
                else:
                    yf[c, :, t] = 2.0 * y - v[c, 0, :, t]
            if step == 0:
                continue
            block = block_of(c, piece)
            for p in range(6):
                even, odd = pair(yf[c, 2 * p, 4 + block], yf[c, 2 * p + 1, 4 + block])
                ro[c, 2 * block, p] = even
                ro[c, 2 * block + 1, p] = odd
            for rel in (0, 1) if piece == 0 else (2,):
                for one in to(c, rel):
                    start(one)
        if step == 0:
            edges(c)
            return
        me = pos[c // 2]
        om[c, me] = yf[c, :, me]
        orr[c, me] = ro[c, me]

    def stage_d(c):
        arrived(om.at[c, 0:3], to_r.at[c, 0])
        arrived(orr.at[c, 0:3], to_r.at[c, 1])

    loads[0].wait()
    prepare(0)
    loads[1].wait()
    pl.semaphore_wait(barrier, len(friends))
    send_in(0)
    for c in (2, 1, 3):
        prepare(c)
        send_in(c)
    loads[2].wait()
    prepare_potential(0)
    send_potential(0)
    prepare_potential(1)
    send_potential(1)
    for one in loads[3:]:
        one.wait()

    stage_a(0)
    stage_b(0, 0)
    stage_a(2)
    stage_b(2, 0)
    stage_a(1)
    stage_b(1, 0, (0, 1))
    stage_a(3)
    stage_b(3, 0)
    finish_potential(0)
    stage_c(0, 0)
    finish_potential(1)
    stage_c(2, 0)
    stage_c(1, 0)
    stage_b(0, 1)
    stage_c(3, 0)
    stage_b(2, 1)
    stage_b(1, 1)
    stage_b(3, 1)
    stage_c(0, 1)
    stage_c(2, 1)
    stage_c(1, 1)
    stage_c(3, 1)
    for c in range(4):
        stage_d(c)
    done = [sm.at[:, 0:3], sr.at[:, 0:3], vp.at[:, :, 0:3], rp.at[:, 0:3], sz, zs, cs, yf.at[:, :, 0:3], ro.at[:, 0:3]]
    for i, ref in enumerate(done):
        copy(ref, ref, sent.at[i], sent.at[i], {"gx": gx}).wait_send()


def place_kernel(om, orr, out_hbm, out, store_s):
    out_rows = out.reshape(2304, 128)
    stores = [pltpu.make_async_copy(out.at[h], out_hbm.at[:, h], store_s.at[h]) for h in range(2)]
    for c in range(4):

        def band(g, carry):
            for x in range(12):
                out_rows[picked(c, g, x, False), :] = om[c, g, x]
            for p in range(6):
                r = orr[c, g, p]
                out_rows[picked(c, g, 2 * p, True), :] = r[0:4]
                out_rows[picked(c, g, 2 * p + 1, True), :] = r[4:8]
            return carry

        lax.fori_loop(0, 4, band, 0)
        if c % 2:
            stores[c // 2].start()
    for one in stores:
        one.wait()


def local(orbitals, potential):
    rows = jnp.transpose(orbitals, (1, 2, 0, 3)).reshape(144, 2, 8, 128)
    pairs = [y_matrices(G02, G12), y_matrices(G12, G02)]
    my1, my2 = (np.stack([p[i] for p in pairs]) for i in range(2))
    hbm = pl.BlockSpec(memory_space=pltpu.HBM)
    chip = pl.BlockSpec(memory_space=pltpu.VMEM)
    tile = (6, 8, 128)
    slab = (12, *tile)
    sem = pltpu.SemaphoreType.DMA

    def vmem(*shape, dtype=F32):
        return pltpu.VMEM(shape, dtype)

    inputs = [rows, potential, jnp.asarray(z_matrices()), jnp.asarray(my1), jnp.asarray(my2)]
    inputs = [pltpu.with_memory_space_constraint(a, pltpu.HBM) for a in inputs]
    main, rest = pl.pallas_call(
        kernel,
        out_shape=[jax.ShapeDtypeStruct((4, 4, 12, 8, 128), F32), jax.ShapeDtypeStruct((4, 4, *tile), F32)],
        in_specs=[hbm] * 5,
        out_specs=[chip] * 2,
        scratch_shapes=[
            vmem(2, 144, 8, 128),
            vmem(12, 12, 128),
            vmem(3, 256, 256, dtype=BF16),
            vmem(2, 96, 144, dtype=BF16),
            vmem(2, 48, 144, dtype=BF16),
            vmem(4, 4, 12, 8, 128),
            vmem(4, 4, *tile),
            vmem(4, 4, 2, 2, 8, 128),
            vmem(2, 12, 8, 128),
            vmem(2, *tile),
            vmem(4, 2, *slab),
            vmem(4, 4, *tile),
            vmem(2, 12, 4, 8, 128),
            vmem(2, *slab),
            vmem(2, 4, *tile),
            vmem(4, 2, 4, 2, 8, 128),
            vmem(4, 2, *tile),
            vmem(4, 2, *tile),
            vmem(4, 2, 2, 2, 6, 3, 8, 128),
            vmem(4, 2, 2, 2, 6, 3, 8, 128),
            vmem(4, *slab),
            vmem(*slab),
            vmem(12, 48, 128, dtype=BF16),
            vmem(12, 48, 128, dtype=BF16),
            vmem(12, 48, 128, dtype=BF16),
            vmem(12, 48, 128, dtype=BF16),
            vmem(576, 256),
            vmem(4, *slab),
            vmem(4, 4, *tile),
            sem((8,)),
            sem((9,)),
            sem((4, 2)),
            sem((2, 3, 2)),
            sem((4,)),
            sem((4, 2)),
            sem((4, 2, 2)),
            sem((4, 2)),
        ],
        compiler_params=pltpu.CompilerParams(
            collective_id=0, has_side_effects=True, vmem_limit_bytes=24 * 1024 * 1024
        ),
    )(*inputs)
    out = pl.pallas_call(
        place_kernel,
        out_shape=jax.ShapeDtypeStruct((144, 2, 8, 128), F32),
        in_specs=[chip] * 2,
        out_specs=hbm,
        scratch_shapes=[vmem(2, 144, 8, 128), sem((2,))],
        compiler_params=pltpu.CompilerParams(vmem_limit_bytes=8 * 1024 * 1024),
    )(main, rest)
    return jnp.transpose(out.reshape(12, 12, 16, 128), (2, 0, 1, 3))


def solution(mesh):
    return jax.shard_map(
        local,
        mesh=mesh,
        in_specs=(P(None, "gx", "gy", "gz"), P("gx", "gy", "gz")),
        out_specs=P(None, "gx", "gy", "gz"),
        check_vma=False,
    )
```

time: 56.1 us -> 47.7 us (0.85)
  Pallas kernels: 53.6 us -> 47.6 us
  local copies, waits for them, and re-layouts: 2.36 us -> 0 us
    pallas_call x1 -> x2, Pallas kernels: 53.6 us -> 47.6 us  [the longest x1 46.2 us: local(): pl.pallas_call(kernel, out_shape=[jax.ShapeDtypeStruct((4, 4, 12, 8, 128)...]
    unnamed x1 -> x0, local copies, waits for them, and re-layouts: 2.36 us -> none
where the time goes in v3:
time: 47.7 us; the launch traced here: 47.6 us
  Pallas kernels  47.6 us (100%)
    pallas_call x1, Pallas kernels, local(): pl.pallas_call(kernel, out_shape=[jax.ShapeDtypeStruct((4, 4, 12, 8, 128)...  46.2 us
    pallas_call x1, Pallas kernels, local(): pl.pallas_call(place_kernel, out_shape=jax.ShapeDtypeStruct((144, 2, 8, 1...  1.36 us

profile of v3, /device:TPU:1, one launch (start us, length us, event | category | flops | bytes accessed | tf_op | source)
XLA Modules:
  0.0 47.6 jit_solution(10081065663711421165)
XLA Ops:
  0.0 46.2 %shard_map.55 = (f32[4,4,12,8,128]{4,3,2,1,0:T(8,128)S(1)}, f32[4,4,6,8,128]{4,3,2,1,0:T(8,128)S(1)}) custom-call(f32[144,2,8,128]{3,2,1,0:T(8,128)} %bitcast.6, f32[12,12,128]{2,1,0:T(8,128)} %pot_hbm.1, bf16[3,256,256]{2,1,0:T(8,128)(2,1)} %constant.6.clone.mz_hbm, bf16[2,96,144]{2,1,0:T(8,128)(2,1)} %constant.7.clone.my1_hbm, ...), custom_call_target="tpu_custom_call" | custom-call | tf_op jit(solution)/shard_map/pallas_call | solution.py:575
  46.2 1.4 %shard_map.56 = f32[144,2,8,128]{3,2,1,0:T(8,128)} custom-call(f32[4,4,12,8,128]{4,3,2,1,0:T(8,128)S(1)} %get-tuple-element.7.om, f32[4,4,6,8,128]{4,3,2,1,0:T(8,128)S(1)} %get-tuple-element.8.orr), custom_call_target="tpu_custom_call" | custom-call | tf_op jit(solution)/shard_map/pallas_call | solution.py:623

commit v4 on v3

--- a/solution.py
+++ b/solution.py
@@ -100,8 +100,7 @@
     mz_hbm,
     my1_hbm,
     my2_hbm,
-    om,
-    orr,
+    out,
     orb,
     pot,
     mz,
@@ -131,6 +130,8 @@
     tz,
     yf,
     ro,
+    om,
+    orr,
     load_s,
     sent,
     tin_r,
@@ -182,7 +183,6 @@
 
     low_half = lax.broadcasted_iota(jnp.int32, (8, 128), 0) < 4
     lane8 = lax.broadcasted_iota(jnp.int32, (8, 128), 1)
-    even_lane = lax.rem(lane8, 12) < 6
     lane = lax.broadcasted_iota(jnp.int32, (48, 128), 1)
 
     def turn(a):
@@ -195,6 +195,7 @@
         return a if by % 128 == 0 else pltpu.roll(a, by % 128, 1)
 
     orb_rows = orb.reshape(2304, 128)
+    out_rows = out.reshape(2304, 128)
     def start(c):
         c.start()
 
@@ -217,20 +218,12 @@
             copy(spr.at[r], rp.at[r, pos[r]], sent.at[3], vin_r.at[r, rel, 1], to),
         ]
 
-    def vpass(r):
-        if r == 0:
-            other, to = near[0][0], {"gy": near[0][2]}
-            return [
-                copy(vp.at[0, :, other], vp.at[0, :, other], sent.at[2], vin_r.at[0, 1, 0], to),
-                copy(rp.at[0, other], rp.at[0, other], sent.at[3], vin_r.at[0, 1, 1], to),
-            ]
-        copies = []
-        for k, (source, target) in enumerate(((1, 2), (2, 1))):
-            other, to = near[1][source], {"gx": near[1][target]}
-            lead, rest = vp.at[1, 6 * k : 6 * k + 6, other], rp.at[1, other, 3 * k : 3 * k + 3]
-            copies.append(copy(lead, lead, sent.at[2], vin_r.at[1, 0, 0], to))
-            copies.append(copy(rest, rest, sent.at[3], vin_r.at[1, 0, 1], to))
-        return copies
+    def vpass():
+        other, to = near[0][0], {"gy": near[0][2]}
+        return [
+            copy(vp.at[0, :, other], vp.at[0, :, other], sent.at[2], vin_r.at[0, 1, 0], to),
+            copy(rp.at[0, other], rp.at[0, other], sent.at[3], vin_r.at[0, 1, 1], to),
+        ]
 
     def zin(c, k, side):
         r = c // 2
@@ -256,20 +249,20 @@
         rp[r, pos[r]] = spr[r]
 
     def send_potential(r):
-        for rel in (r, 2):
+        for rel in ((0, 2), (1, 2, 0))[r]:
             for one in vin(r, rel):
                 start(one)
 
-    def pass_potential(r):
-        for rel in (r, 2):
-            for one in vin(r, rel):
+    def pass_potential():
+        for rel in (0, 2):
+            for one in vin(0, rel):
                 one.wait_recv()
-        for one in vpass(r):
+        for one in vpass():
             start(one)
 
     def finish_potential(r):
-        arrived(vp.at[r, :, 0], vin_r.at[r, 1 - r, 0])
-        arrived(rp.at[r, 0], vin_r.at[r, 1 - r, 1])
+        for one in vpass() if r == 0 else vin(1, 0) + vin(1, 1) + vin(1, 2):
+            one.wait_recv()
 
         def scaled(a):
             return (a - CENTER) * (1.0 / HALF_WIDTH) + 3.0 * XC[0]
@@ -283,27 +276,23 @@
 
     def prepare(c):
         def band(g, carry):
-            main = [None] * 2
-            rest = [None] * 4
+            edge = [None] * 2
             for x in range(12):
                 val = orb_rows[picked(c, g, x, False), :]
                 sm[c, g, x] = val
                 for side in range(2):
                     r = lanes(val, 6 * x + 6 * side)
-                    main[side] = r if x == 0 else jnp.where(lane8 >= 6 * x, r, main[side])
+                    edge[side] = r if x == 0 else jnp.where(lane8 >= 6 * x, r, edge[side])
             for p in range(6):
                 lo = orb_rows[picked(c, g, 2 * p, True), :]
                 hi = orb_rows[picked(c, g, 2 * p + 1, True), :]
                 val = jnp.concatenate([lo, hi], axis=0)
                 sr[c, g, p] = val
                 for side in range(2):
-                    for odd in range(2):
-                        r = lanes(val, 12 * p + 6 * odd + 6 * side)
-                        at = 2 * side + odd
-                        rest[at] = r if p == 0 else jnp.where(lane8 >= 12 * p + 6 * odd, r, rest[at])
+                    r = lanes(val, 72 + 6 * p + 6 * side)
+                    edge[side] = jnp.where(lane8 >= 72 + 6 * p, r, edge[side])
             for side in range(2):
-                sz[c, g, side, 0] = main[side]
-                sz[c, g, side, 1] = jnp.where(low_half, rest[2 * side], rest[2 * side + 1])
+                sz[c, g, side] = edge[side]
             return carry
 
         lax.fori_loop(0, 4, band, 0)
@@ -361,20 +350,27 @@
             side_at[c // 2][side],
         )
 
-    def halo(c, step, side):
+    def halo(c, step):
         if step == 1:
-            zx(c, 1 - side).wait_recv()
-            return zr[c, side].reshape(48, 128)
-        if side == 0:
-            arrived(zd.at[c], zd_r.at[c])
-        tiles = [zd[c, side, s, 0] for s in range(4)]
-        for t in range(2):
-            a = zd[c, side, 2 * t, 1]
-            b = zd[c, side, 2 * t + 1, 1]
-            a = jnp.where(even_lane, a, turn(a))
-            b = jnp.where(even_lane, turn(b), b)
-            tiles.append(jnp.where(low_half, a, b))
-        return jnp.concatenate(tiles, axis=0)
+            for side in range(2):
+                zx(c, side).wait_recv()
+            far_side = [zr[c, side].reshape(48, 128) for side in range(2)]
+            return lambda side, x, by: lanes(far_side[side], by - 6 * x)
+        arrived(zd.at[c], zd_r.at[c])
+        main = []
+        rest = []
+        for side in range(2):
+            tiles = [zd[c, side, s] for s in range(4)]
+            main.append(jnp.concatenate(tiles, axis=0))
+            both = [pair(tiles[2 * t], tiles[2 * t + 1]) for t in range(2)]
+            rest.append([jnp.concatenate([both[0][k], both[1][k]], axis=0) for k in range(2)])
+
+        def edge(side, x, by):
+            a = lanes(main[side], by - 6 * x)
+            b = lanes(rest[side][x % 2], by - 72 - 6 * (x // 2))
+            return jnp.concatenate([a, b], axis=0)
+
+        return edge
 
     def block_of(c, piece):
         return far[c // 2] if piece == 0 else half[c // 2]
@@ -383,16 +379,15 @@
         block = block_of(c, piece)
         return 2 * block + i if i < 2 else 4 + block
 
-    def stage_b(c, step, between=()):
+    def stage_b(c, step):
         for x in range(12):
             a, b = split(v[c, step, x].reshape(48, 128))
             v1[x] = a
             v2[x] = b
-        below = halo(c, step, 0)
-        above = halo(c, step, 1)
+        edge = halo(c, step)
         for x in range(12):
-            up = lanes(above, 128 - 6 * x)
-            down = lanes(below, 122 - 6 * x)
+            up = edge(1, x, 128)
+            down = edge(0, x, 122)
             h = jnp.where(lane < 6, up, jnp.where(lane >= 122, down, 0.0))
             a, b = split(h)
             h1[x] = a
@@ -422,8 +417,6 @@
                 wf[x] = w[:, 128 * i : 128 * i + 128].reshape(6, 8, 128)
                 part[c, x] = r[:, 128 * i : 128 * i + 128].reshape(6, 8, 128)
 
-        for r in between:
-            pass_potential(r)
         for piece in range(2):
             block = block_of(c, piece)
 
@@ -446,7 +439,7 @@
                     part[c, j, t] = part[c, j, t] + acc[6 + j]
                 return carry
 
-            lax.fori_loop(0, 3, tile, 0)
+            lax.fori_loop(0, 3, tile, 0, unroll=True)
             for side in range(2):
                 start(xc(c, step, side, piece))
 
@@ -491,6 +484,17 @@
         arrived(om.at[c, 0:3], to_r.at[c, 0])
         arrived(orr.at[c, 0:3], to_r.at[c, 1])
 
+        def band(g, carry):
+            for x in range(12):
+                out_rows[picked(c, g, x, False), :] = om[c, g, x]
+            for p in range(6):
+                r = orr[c, g, p]
+                out_rows[picked(c, g, 2 * p, True), :] = r[0:4]
+                out_rows[picked(c, g, 2 * p + 1, True), :] = r[4:8]
+            return carry
+
+        lax.fori_loop(0, 4, band, 0)
+
     loads[0].wait()
     prepare(0)
     loads[1].wait()
@@ -503,56 +507,48 @@
     prepare_potential(0)
     send_potential(0)
     prepare_potential(1)
-    send_potential(1)
     for one in loads[3:]:
         one.wait()
 
+    send_potential(1)
     stage_a(0)
     stage_b(0, 0)
     stage_a(2)
     stage_b(2, 0)
     stage_a(1)
-    stage_b(1, 0, (0, 1))
+    stage_b(1, 0)
+    pass_potential()
     stage_a(3)
     stage_b(3, 0)
     finish_potential(0)
-    stage_c(0, 0)
     finish_potential(1)
     stage_c(2, 0)
+    stage_c(0, 0)
+    stage_c(3, 0)
+    stage_b(2, 1)
     stage_c(1, 0)
     stage_b(0, 1)
-    stage_c(3, 0)
-    stage_b(2, 1)
+    stage_b(3, 1)
     stage_b(1, 1)
-    stage_b(3, 1)
+    stage_c(2, 1)
     stage_c(0, 1)
-    stage_c(2, 1)
+    stage_c(3, 1)
     stage_c(1, 1)
-    stage_c(3, 1)
-    for c in range(4):
+    for c in (2, 0, 3, 1):
         stage_d(c)
     done = [sm.at[:, 0:3], sr.at[:, 0:3], vp.at[:, :, 0:3], rp.at[:, 0:3], sz, zs, cs, yf.at[:, :, 0:3], ro.at[:, 0:3]]
     for i, ref in enumerate(done):
         copy(ref, ref, sent.at[i], sent.at[i], {"gx": gx}).wait_send()
 
 
-def place_kernel(om, orr, out_hbm, out, store_s):
-    out_rows = out.reshape(2304, 128)
-    stores = [pltpu.make_async_copy(out.at[h], out_hbm.at[:, h], store_s.at[h]) for h in range(2)]
-    for c in range(4):
-
-        def band(g, carry):
-            for x in range(12):
-                out_rows[picked(c, g, x, False), :] = om[c, g, x]
-            for p in range(6):
-                r = orr[c, g, p]
-                out_rows[picked(c, g, 2 * p, True), :] = r[0:4]
-                out_rows[picked(c, g, 2 * p + 1, True), :] = r[4:8]
-            return carry
-
-        lax.fori_loop(0, 4, band, 0)
-        if c % 2:
-            stores[c // 2].start()
+def place_kernel(out, out_hbm, store_s):
+    stores = [
+        pltpu.make_async_copy(out.at[h, 36 * k : 36 * k + 36], out_hbm.at[36 * k : 36 * k + 36, h], store_s.at[h, k])
+        for h in range(2)
+        for k in range(4)
+    ]
+    for one in stores:
+        one.start()
     for one in stores:
         one.wait()
 
@@ -572,11 +568,11 @@
 
     inputs = [rows, potential, jnp.asarray(z_matrices()), jnp.asarray(my1), jnp.asarray(my2)]
     inputs = [pltpu.with_memory_space_constraint(a, pltpu.HBM) for a in inputs]
-    main, rest = pl.pallas_call(
+    placed = pl.pallas_call(
         kernel,
-        out_shape=[jax.ShapeDtypeStruct((4, 4, 12, 8, 128), F32), jax.ShapeDtypeStruct((4, 4, *tile), F32)],
+        out_shape=jax.ShapeDtypeStruct((2, 144, 8, 128), F32),
         in_specs=[hbm] * 5,
-        out_specs=[chip] * 2,
+        out_specs=chip,
         scratch_shapes=[
             vmem(2, 144, 8, 128),
             vmem(12, 12, 128),
@@ -585,7 +581,7 @@
             vmem(2, 48, 144, dtype=BF16),
             vmem(4, 4, 12, 8, 128),
             vmem(4, 4, *tile),
-            vmem(4, 4, 2, 2, 8, 128),
+            vmem(4, 4, 2, 8, 128),
             vmem(2, 12, 8, 128),
             vmem(2, *tile),
             vmem(4, 2, *slab),
@@ -593,7 +589,7 @@
             vmem(2, 12, 4, 8, 128),
             vmem(2, *slab),
             vmem(2, 4, *tile),
-            vmem(4, 2, 4, 2, 8, 128),
+            vmem(4, 2, 4, 8, 128),
             vmem(4, 2, *tile),
             vmem(4, 2, *tile),
             vmem(4, 2, 2, 2, 6, 3, 8, 128),
@@ -606,6 +602,8 @@
             vmem(12, 48, 128, dtype=BF16),
             vmem(576, 256),
             vmem(4, *slab),
+            vmem(4, 4, *tile),
+            vmem(4, 4, 12, 8, 128),
             vmem(4, 4, *tile),
             sem((8,)),
             sem((9,)),
@@ -623,11 +621,11 @@
     out = pl.pallas_call(
         place_kernel,
         out_shape=jax.ShapeDtypeStruct((144, 2, 8, 128), F32),
-        in_specs=[chip] * 2,
+        in_specs=[chip],
         out_specs=hbm,
-        scratch_shapes=[vmem(2, 144, 8, 128), sem((2,))],
+        scratch_shapes=[sem((2, 4))],
         compiler_params=pltpu.CompilerParams(vmem_limit_bytes=8 * 1024 * 1024),
-    )(main, rest)
+    )(placed)
     return jnp.transpose(out.reshape(12, 12, 16, 128), (2, 0, 1, 3))
 
 

time: 47.7 us -> 47 us (0.985)
  Pallas kernels: 47.6 us -> 46.8 us
where the time goes in v4:
time: 47 us; the launch traced here: 46.8 us
  Pallas kernels  46.8 us (100%)
    pallas_call x1, Pallas kernels, local(): pl.pallas_call(kernel, out_shape=jax.ShapeDtypeStruct((2, 144, 8, 128), F...  45.8 us
    pallas_call x1, Pallas kernels, local(): pl.pallas_call(place_kernel, out_shape=jax.ShapeDtypeStruct((144, 2, 8, 1...  1.07 us

profile of v4, /device:TPU:1, one launch (start us, length us, event | category | flops | bytes accessed | tf_op | source)
XLA Modules:
  0.0 46.8 jit_solution(17762932362801120069)
XLA Ops:
  0.0 45.8 %shard_map.55.out = f32[2,144,8,128]{3,2,1,0:T(8,128)S(1)} custom-call(f32[144,2,8,128]{3,2,1,0:T(8,128)} %bitcast.6, f32[12,12,128]{2,1,0:T(8,128)} %pot_hbm.1, bf16[3,256,256]{2,1,0:T(8,128)(2,1)} %constant.6.clone.mz_hbm, bf16[2,96,144]{2,1,0:T(8,128)(2,1)} %constant.7.clone.my1_hbm, bf16[2,48,144]{2,1,0:T(8,128)(2,1)} %constant.8.clone.my2_hbm), custom_call_target="tpu_custom_call" | custom-call | tf_op jit(solution)/shard_map/pallas_call | solution.py:571
  45.8 1.1 %shard_map.56 = f32[144,2,8,128]{3,2,1,0:T(8,128)} custom-call(f32[2,144,8,128]{3,2,1,0:T(8,128)S(1)} %shard_map.55.out), custom_call_target="tpu_custom_call" | custom-call | tf_op jit(solution)/shard_map/pallas_call | solution.py:621

commit v5 on v4

--- a/solution.py
+++ b/solution.py
@@ -384,6 +384,14 @@
             a, b = split(v[c, step, x].reshape(48, 128))
             v1[x] = a
             v2[x] = b
+        for xp in range(6):
+            x0, x1 = 2 * xp, 2 * xp + 1
+            a = jnp.concatenate([v1[x0], v1[x1]], axis=1)
+            b = jnp.concatenate([v2[x0], v2[x1]], axis=1)
+            q = jnp.dot(my1[c // 2], jnp.concatenate([a, b, a], axis=0), preferred_element_type=F32)
+            for i, x in enumerate((x0, x1)):
+                wf[x] = q[0:48, 128 * i : 128 * i + 128].reshape(6, 8, 128)
+                part[c, x] = q[48:96, 128 * i : 128 * i + 128].reshape(6, 8, 128)
         edge = halo(c, step)
         for x in range(12):
             up = edge(1, x, 128)
@@ -404,18 +412,14 @@
             tz[288 * part_rows : 288 * part_rows + 288] = acc
         for xp in range(6):
             x0, x1 = 2 * xp, 2 * xp + 1
-            a = jnp.concatenate([v1[x0], v1[x1]], axis=1)
-            b = jnp.concatenate([v2[x0], v2[x1]], axis=1)
-            q = jnp.dot(my1[c // 2], jnp.concatenate([a, b, a], axis=0), preferred_element_type=F32)
             t = jnp.concatenate([tz[48 * x0 : 48 * x0 + 48, 0:128], tz[48 * x1 : 48 * x1 + 48, 0:128]], axis=1)
             s = jnp.concatenate([tz[48 * x0 : 48 * x0 + 48, 128:256], tz[48 * x1 : 48 * x1 + 48, 128:256]], axis=1)
             ta, tb = split(t)
             r = jnp.dot(my2[c // 2], jnp.concatenate([ta, tb, ta], axis=0), preferred_element_type=F32)
-            w = q[0:48] + t
-            r = r + q[48:96] + s
+            r = r + s
             for i, x in enumerate((x0, x1)):
-                wf[x] = w[:, 128 * i : 128 * i + 128].reshape(6, 8, 128)
-                part[c, x] = r[:, 128 * i : 128 * i + 128].reshape(6, 8, 128)
+                wf[x] = wf[x] + t[:, 128 * i : 128 * i + 128].reshape(6, 8, 128)
+                part[c, x] = part[c, x] + r[:, 128 * i : 128 * i + 128].reshape(6, 8, 128)
 
         for piece in range(2):
             block = block_of(c, piece)

time: 47 us -> 47.1 us (level)
  no operation moved by 1% of the time
where the time goes in v5:
time: 47.1 us; the launch traced here: 47 us
  Pallas kernels  47 us (100%)
    pallas_call x1, Pallas kernels, local(): pl.pallas_call(kernel, out_shape=jax.ShapeDtypeStruct((2, 144, 8, 128), F...  45.9 us
    pallas_call x1, Pallas kernels, local(): pl.pallas_call(place_kernel, out_shape=jax.ShapeDtypeStruct((144, 2, 8, 1...  1.07 us

profile of v5, /device:TPU:1, one launch (start us, length us, event | category | flops | bytes accessed | tf_op | source)
XLA Modules:
  0.0 47.0 jit_solution(834167034970846154)
XLA Ops:
  0.0 45.9 %shard_map.55.out = f32[2,144,8,128]{3,2,1,0:T(8,128)S(1)} custom-call(f32[144,2,8,128]{3,2,1,0:T(8,128)} %bitcast.6, f32[12,12,128]{2,1,0:T(8,128)} %pot_hbm.1, bf16[3,256,256]{2,1,0:T(8,128)(2,1)} %constant.6.clone.mz_hbm, bf16[2,96,144]{2,1,0:T(8,128)(2,1)} %constant.7.clone.my1_hbm, bf16[2,48,144]{2,1,0:T(8,128)(2,1)} %constant.8.clone.my2_hbm), custom_call_target="tpu_custom_call" | custom-call | tf_op jit(solution)/shard_map/pallas_call | solution.py:575
  45.9 1.1 %shard_map.56 = f32[144,2,8,128]{3,2,1,0:T(8,128)} custom-call(f32[2,144,8,128]{3,2,1,0:T(8,128)S(1)} %shard_map.55.out), custom_call_target="tpu_custom_call" | custom-call | tf_op jit(solution)/shard_map/pallas_call | solution.py:625

commit v6 on v4

--- a/solution.py
+++ b/solution.py
@@ -511,15 +511,15 @@
         one.wait()
 
     send_potential(1)
+    stage_a(2)
+    stage_b(2, 0)
     stage_a(0)
     stage_b(0, 0)
-    stage_a(2)
-    stage_b(2, 0)
+    stage_a(3)
+    stage_b(3, 0)
+    pass_potential()
     stage_a(1)
     stage_b(1, 0)
-    pass_potential()
-    stage_a(3)
-    stage_b(3, 0)
     finish_potential(0)
     finish_potential(1)
     stage_c(2, 0)

time: 47 us -> 47 us (level)
  no operation moved by 1% of the time
where the time goes in v6:
time: 47 us; the launch traced here: 46.8 us
  Pallas kernels  46.8 us (100%)
    pallas_call x1, Pallas kernels, local(): pl.pallas_call(kernel, out_shape=jax.ShapeDtypeStruct((2, 144, 8, 128), F...  45.7 us
    pallas_call x1, Pallas kernels, local(): pl.pallas_call(place_kernel, out_shape=jax.ShapeDtypeStruct((144, 2, 8, 1...  1.07 us

profile of v6, /device:TPU:1, one launch (start us, length us, event | category | flops | bytes accessed | tf_op | source)
XLA Modules:
  0.0 46.8 jit_solution(12111768581498461371)
XLA Ops:
  0.0 45.7 %shard_map.55.out = f32[2,144,8,128]{3,2,1,0:T(8,128)S(1)} custom-call(f32[144,2,8,128]{3,2,1,0:T(8,128)} %bitcast.6, f32[12,12,128]{2,1,0:T(8,128)} %pot_hbm.1, bf16[3,256,256]{2,1,0:T(8,128)(2,1)} %constant.6.clone.mz_hbm, bf16[2,96,144]{2,1,0:T(8,128)(2,1)} %constant.7.clone.my1_hbm, bf16[2,48,144]{2,1,0:T(8,128)(2,1)} %constant.8.clone.my2_hbm), custom_call_target="tpu_custom_call" | custom-call | tf_op jit(solution)/shard_map/pallas_call | solution.py:571
  45.7 1.1 %shard_map.56 = f32[144,2,8,128]{3,2,1,0:T(8,128)} custom-call(f32[2,144,8,128]{3,2,1,0:T(8,128)S(1)} %shard_map.55.out), custom_call_target="tpu_custom_call" | custom-call | tf_op jit(solution)/shard_map/pallas_call | solution.py:621
